TPU v7x, 512 devices: a whole 4x4x16 slice. The times are simulated.
512 devices in a mesh: fsdp: 16 (over x, z_hi), tensor: 8 (over z_lo, core), pool: 4 (over y).
Axes of the slice: x: 4, y: 4, z: 16 (z_hi: 4, z_lo: 4; z = z_hi * 4 + z_lo), core: 2. Of those that a mesh axis runs over, the one named last changes fastest.
Arguments:
- hidden: bfloat16 [32768, 5120], P(('fsdp', 'pool'), 'tensor'), may hold values from -6 to 6
- queries: bfloat16 [32768, 5120], P(('fsdp', 'pool'), 'tensor'), may hold values from -200 to 200
- cotangent: bfloat16 [32768, 5120], P(('fsdp', 'pool'), 'tensor'), may hold values from -6 to 6
- segment: int32 [64, 512], P(('fsdp', 'pool')), may hold values from 0 to 15, never falling along the last dimension, each value on 1 to 384 neighbouring positions
- clip_mask: int32 [32768], P(('fsdp', 'pool')), may hold values 0 or 1
- rewards: float32 [1024], P(('fsdp', 'pool')), may hold values from 0 to 1
- seq_order: int32 [1024], P(('fsdp', 'pool')), may hold values from 0 to 1023, each once
- kv_weight: float32 [5120, 2, 1024], P('fsdp', None, 'tensor'), may hold values from -0.078125 to 0.078125
- moment_one: float32 [5120, 2, 1024], P('fsdp', None, 'tensor'), may hold values from -60 to 60
- moment_two: float32 [5120, 2, 1024], P('fsdp', None, 'tensor'), may hold values from 1 to 10000
- dec_hidden: bfloat16 [512, 4, 5120], P(('fsdp', 'pool')), may hold values from -6 to 6
- dec_queries: bfloat16 [512, 4, 5120], P(('fsdp', 'pool'), None, 'tensor'), may hold values from -200 to 200
- kv_cache: bfloat16 [512, 256, 2, 1024], P(('fsdp', 'pool'), None, None, 'tensor'), may hold values from -6 to 6
- cache_len: int32 [512], P(('fsdp', 'pool')), may hold values from 1 to 256
Outputs:
- new_weight: float32 [5120, 2, 1024], P('fsdp', None, 'tensor')
- new_moment_one: float32 [5120, 2, 1024], P('fsdp', None, 'tensor')
- new_moment_two: float32 [5120, 2, 1024], P('fsdp', None, 'tensor')
- dec_out: bfloat16 [512, 4, 5120], P(('fsdp', 'pool'), None, 'tensor')
Inputs may be any that keep to these rules, and one draw needn't show every extreme that they name: `segment`: each row never falls; every sequence number of a row has 1 to 384 tokens. `seq_order`: each place once.
All inputs are finite; a program needn't handle non-finite values. No bound on the sum of `clip_mask` on one device may be relied on, other than what follows from the above.
Results may differ from a plain program's by a relative error of at most 0.014.
The roundings to bfloat16 on the way count: a program that leaves them out, or rounds other values in their place, can miss the bound.
Values may be sent and summed in bfloat16 or wider, within the bound.
A program may use at most 64 MiB of HBM per device.

v0:
```python
import math

import jax
import jax.numpy as jnp
from jax import lax
from jax.sharding import Mesh
from jax.sharding import PartitionSpec as P

D = 5120
QH = 40
KVH = 8
HD = 128
GROUP = 16
FSDP = ("fsdp_0", "fsdp_1")
FSDP_POOL = ("fsdp_0", "fsdp_1", "pool")


beta_one = 0.9
beta_two = 0.999
learn_rate = 0.001
weight_decay = 0.1
adam_epsilon = 1e-08
adam_step = 10.0
variance_floor = 0.04
masked_score = -1e30


def from_everyone(shard, axis):
    count = lax.axis_size(axis)
    return lax.all_to_all(
        jnp.broadcast_to(shard[None], (count, *shard.shape)), axis, 0, 0, tiled=True
    )


def of_everyone(shard, axis):
    everything = from_everyone(shard, axis)
    return jnp.sum(everything, axis=0)


def sum_by_axis(terms, axes):
    so_far = terms.astype(jnp.bfloat16)
    for axis in axes:
        so_far = lax.psum_scatter(so_far, axis, scatter_dimension=0, tiled=True)
    return so_far.astype(jnp.float32)


def cut_along(shard, dim, count):
    before, after = (shard.shape[:dim], shard.shape[dim + 1 :])
    return jnp.moveaxis(shard.reshape(*before, count, -1, *after), dim, 0)


def summed_on_arrival(shard, axis, dim):
    pieces = cut_along(shard, dim, lax.axis_size(axis))
    arrived = lax.all_to_all(pieces, axis, split_axis=0, concat_axis=0, tiled=True)
    return arrived.sum(axis=0)


def learner_grads(keys_values, queries, cotangent, segment, coefficient):
    block_rows = queries.shape[0]
    head_size = queries.shape[3]
    score_scale = 1.0 / math.sqrt(head_size)
    key_rows = keys_values[:, 0]
    value_rows = keys_values[:, 1]
    scores = (
        jnp.einsum("thrd,uhd->hrtu", queries, key_rows, preferred_element_type=jnp.float32)
        * score_scale
    )
    places = jnp.arange(block_rows)
    allowed = (segment[:, None] == segment[None, :]) & (places[None, :] <= places[:, None])
    scores = jnp.where(allowed, scores, masked_score)
    row_max = jnp.max(scores, axis=-1, keepdims=True)
    weights = jnp.exp(scores - row_max)
    attention = weights / jnp.sum(weights, axis=-1, keepdims=True)
    attention_low = attention.astype(jnp.bfloat16)
    upstream = (coefficient[:, None, None, None] * cotangent.astype(jnp.float32)).astype(
        jnp.bfloat16
    )
    grad_prob = jnp.einsum(
        "thrd,uhd->hrtu", upstream, value_rows, preferred_element_type=jnp.float32
    )
    row_inner = jnp.sum(attention * grad_prob, axis=-1, keepdims=True)
    grad_score = (attention * (grad_prob - row_inner) * score_scale).astype(jnp.bfloat16)
    grad_values = jnp.einsum(
        "hrtu,thrd->uhd", attention_low, upstream, preferred_element_type=jnp.float32
    )
    grad_keys = jnp.einsum(
        "hrtu,thrd->uhd", grad_score, queries, preferred_element_type=jnp.float32
    )
    return jnp.stack([grad_keys, grad_values], axis=1).astype(jnp.bfloat16)


def decode_attend(queries, cache, fresh, lengths):
    head_size = queries.shape[4]
    steps_here = queries.shape[1]
    capacity = cache.shape[1]
    score_scale = 1.0 / math.sqrt(head_size)
    cached = (
        jnp.einsum("bshqd,blhd->bshql", queries, cache[:, :, 0], preferred_element_type=jnp.float32)
        * score_scale
    )
    recent = (
        jnp.einsum("bshqd,bjhd->bshqj", queries, fresh[:, :, 0], preferred_element_type=jnp.float32)
        * score_scale
    )
    live = jnp.arange(capacity)[None, :] < lengths[:, None]
    cached = jnp.where(live[:, None, None, None, :], cached, masked_score)
    before = jnp.arange(steps_here)[None, :] <= jnp.arange(steps_here)[:, None]
    recent = jnp.where(before[None, :, None, None, :], recent, masked_score)
    row_max = jnp.maximum(
        jnp.max(cached, axis=-1, keepdims=True), jnp.max(recent, axis=-1, keepdims=True)
    )
    cached_exp = jnp.exp(cached - row_max)
    recent_exp = jnp.exp(recent - row_max)
    total = jnp.sum(cached_exp, axis=-1, keepdims=True) + jnp.sum(
        recent_exp, axis=-1, keepdims=True
    )
    cached_low = (cached_exp / total).astype(jnp.bfloat16)
    recent_low = (recent_exp / total).astype(jnp.bfloat16)
    output = jnp.einsum(
        "bshql,blhd->bshqd", cached_low, cache[:, :, 1], preferred_element_type=jnp.float32
    )
    output = output + jnp.einsum(
        "bshqj,bjhd->bshqd", recent_low, fresh[:, :, 1], preferred_element_type=jnp.float32
    )
    return output.astype(jnp.bfloat16).reshape(queries.shape[0], steps_here, -1)


def body(
    hidden,
    queries,
    cotangent,
    segment,
    clip_mask,
    rewards,
    seq_order,
    kv_weight,
    moment_one,
    moment_two,
    dec_hidden,
    dec_queries,
    kv_cache,
    cache_len,
):
    block_rows = hidden.shape[0]
    kv_width = kv_weight.shape[2]
    heads_here = kv_width // HD
    head_ratio = QH // KVH
    weight_low = kv_weight.astype(jnp.bfloat16)
    weight_full = lax.all_gather(weight_low, FSDP, axis=0, tiled=True)
    tokens_full = lax.all_gather(hidden, "tensor", axis=1, tiled=True)
    projected = jnp.dot(
        tokens_full, weight_full.reshape(D, 2 * kv_width), preferred_element_type=jnp.float32
    )
    keys_values = projected.astype(jnp.bfloat16).reshape(block_rows, 2, heads_here, HD)
    shards = lax.axis_size(FSDP) * lax.axis_size("pool")
    groups_total = rewards.shape[0] * shards // GROUP
    group_of = seq_order // GROUP
    onehot = (group_of[:, None] == jnp.arange(groups_total, dtype=jnp.int32)[None, :]).astype(
        jnp.float32
    )
    stats = jnp.stack([rewards, rewards * rewards], axis=1)
    partial_sums = jnp.sum(onehot[:, :, None] * stats[:, None, :], axis=0)
    sums = of_everyone(partial_sums, FSDP_POOL)
    mean = sums[:, 0] / GROUP
    spread = sums[:, 1] / GROUP - mean * mean
    denom = jnp.sqrt(jnp.maximum(spread, variance_floor))
    advantage = (rewards - jnp.sum(onehot * mean[None, :], axis=1)) / jnp.sum(
        onehot * denom[None, :], axis=1
    )
    local_seg = segment[0]
    member = (local_seg[:, None] == jnp.arange(rewards.shape[0], dtype=jnp.int32)[None, :]).astype(
        jnp.float32
    )
    coefficient = jnp.sum(member * advantage[None, :], axis=1) * clip_mask.astype(jnp.float32)
    query_rows = queries.reshape(block_rows, heads_here, head_ratio, HD)
    cot_rows = cotangent.reshape(block_rows, heads_here, head_ratio, HD)
    grad_kv = learner_grads(keys_values, query_rows, cot_rows, local_seg, coefficient).reshape(
        block_rows, 2 * kv_width
    )
    partial_value = jnp.einsum(
        "tc,tk->ck", tokens_full, grad_kv, preferred_element_type=jnp.float32
    )
    shard_grad = sum_by_axis(
        partial_value.reshape(kv_weight.shape[0] * lax.axis_size(FSDP), 2, kv_width), FSDP
    )
    grad = of_everyone(shard_grad, "pool")
    new_moment_one = beta_one * moment_one + (1.0 - beta_one) * grad
    new_moment_two = beta_two * moment_two + (1.0 - beta_two) * grad * grad
    first_hat = new_moment_one / (1.0 - beta_one**adam_step)
    second_hat = new_moment_two / (1.0 - beta_two**adam_step)
    new_weight = kv_weight - learn_rate * (
        first_hat / (jnp.sqrt(second_hat) + adam_epsilon) + weight_decay * kv_weight
    )
    dec_rows = dec_hidden.shape[0]
    steps_here = dec_hidden.shape[1]
    capacity = kv_cache.shape[1]
    rollout_low = new_weight.astype(jnp.bfloat16)
    columns = lax.all_to_all(dec_hidden, FSDP, split_axis=2, concat_axis=0, tiled=True)
    piece_width = columns.shape[2]
    rollout_flat = rollout_low.reshape(piece_width, 2 * kv_width)
    product = jnp.dot(
        columns.reshape(dec_rows * lax.axis_size(FSDP) * steps_here, piece_width),
        rollout_flat,
        preferred_element_type=jnp.float32,
    )
    fresh = summed_on_arrival(
        product.reshape(dec_rows * lax.axis_size(FSDP), steps_here, 2 * kv_width), FSDP, 0
    )
    fresh_low = fresh.astype(jnp.bfloat16).reshape(dec_rows, steps_here, 2, heads_here, HD)
    cache = kv_cache.reshape(dec_rows, capacity, 2, heads_here, HD)
    query_dec = dec_queries.reshape(dec_rows, steps_here, heads_here, head_ratio, HD)
    dec_out = decode_attend(query_dec, cache, fresh_low, cache_len)
    return (new_weight, new_moment_one, new_moment_two, dec_out)


def solution(mesh):
    finer = Mesh(
        mesh.devices.reshape(4, 4, mesh.shape["tensor"], mesh.shape["pool"]),
        ("fsdp_0", "fsdp_1", "tensor", "pool"),
    )
    in_specs = (
        P(FSDP_POOL, "tensor"),
        P(FSDP_POOL, "tensor"),
        P(FSDP_POOL, "tensor"),
        P(FSDP_POOL, None),
        P(FSDP_POOL),
        P(FSDP_POOL),
        P(FSDP_POOL),
        P(FSDP, None, "tensor"),
        P(FSDP, None, "tensor"),
        P(FSDP, None, "tensor"),
        P(FSDP_POOL, None, None),
        P(FSDP_POOL, None, "tensor"),
        P(FSDP_POOL, None, None, "tensor"),
        P(FSDP_POOL),
    )
    out_specs = (
        P(FSDP, None, "tensor"),
        P(FSDP, None, "tensor"),
        P(FSDP, None, "tensor"),
        P(FSDP_POOL, None, "tensor"),
    )
    return jax.shard_map(body, mesh=finer, in_specs=in_specs, out_specs=out_specs, check_vma=False)
```

profile of v0, /device:TPU:1, one launch (start us, length us, event | category | flops | bytes accessed | tf_op | source)
XLA Modules:
  0.0 462.3 jit_solution(10101156402707544405)
XLA Ops:
  7.2 1.8 convert_element_type.98
  9.0 0.7 all-gather.3.cloned.1.call-update
  9.7 0.7 multiply_bitcast_fusion.1
  10.4 0.7 pad_maximum_fusion.1
  11.1 0.7 and_select_fusion
  11.9 0.7 reshape.300
  12.6 21.7 %all-to-all-start = ((f32[64,1,128]{2,1,0:T(1,128)}), f32[64,1,128]{2,1,0:T(1,128)S(1)}, u32[]{:S(2)}, u32[]{:S(2)}) async-start(f32[64,1,128]{2,1,0:T(1,128)} %reshape.300), calls=%async_computation | async-start | bytes 65536 | tf_op jit(solution)/shard_map/all_to_all | solution.py:30
  34.4 1.3 copy.154
  35.8 1.3 copy.157
  37.1 1.0 fusion.49
  38.1 11.9 %all-to-all-done = f32[64,1,128]{2,1,0:T(1,128)S(1)} async-done(((f32[64,1,128]{2,1,0:T(1,128)}), f32[64,1,128]{2,1,0:T(1,128)S(1)}, u32[]{:S(2)}, u32[]{:S(2)}) %all-to-all-start) | async-done | bytes 32800 | tf_op jit(solution)/shard_map/all_to_all | solution.py:30
  50.0 0.5 broadcast.178
  50.5 0.7 reduce.7
  51.6 0.7 subtract_divide_fusion
  52.2 0.8 select_reduce_fusion
  53.0 0.7 convert_multiply_fusion
  53.8 68.1 %all-gather.5.cloned.1.call-done = bf16[5120,2,128]{2,1,0:T(2,128)(2,1)} async-done(((bf16[320,2,128]{2,1,0:T(2,128)(2,1)}), bf16[5120,2,128]{2,1,0:T(2,128)(2,1)}) %all-gather.5.cloned.1.call-update) | async-done | bytes 2621456 | tf_op jit(solution)/shard_map/all_gather | solution.py:149
  122.0 66.0 %all-gather.3.cloned.1.call-done = bf16[512,5120]{1,0:T(8,128)(2,1)} async-done(((bf16[512,640]{1,0:T(8,128)(2,1)}), bf16[512,5120]{1,0:T(8,128)(2,1)}) %all-gather.3.cloned.1.call-update) | async-done | bytes 5242896 | tf_op jit(solution)/shard_map/all_gather | solution.py:150
  187.9 4.9 %fusion.20 = bf16[512,256]{0,1:T(8,128)(2,1)S(1)} fusion(bf16[512,5120]{1,0:T(8,128)(2,1)} %all-gather.3.cloned.1.call-done, bf16[640,8,2,128]{3,2,1,0:T(2,128)(2,1)} %bitcast.254), kind=kOutput, calls=%fused_computation.25 | convolution fusion | flops 1342308352 | bytes 8126464 | tf_op jit(solution)/shard_map/dot_general | solution.py:151
  192.8 1.1 fusion.6
  193.9 1.1 fusion.5
  195.0 1.7 fusion.39
  196.7 1.9 fusion
  198.6 2.4 fusion.42
  201.2 1.6 convolution_convert_fusion
  202.8 4.7 %copy.161 = bf16[5120,2,128]{2,1,0:T(2,128)(2,1)} copy(bf16[5120,2,128]{0,2,1:T(8,128)(2,1)S(1)} %bitcast.240) | data formatting | bytes 5242880 | tf_op jit(solution)/shard_map/convert_element_type | solution.py:41
  207.5 5.0 %copy.170 = bf16[8,4,5120]{0,1,2:T(4,128)(2,1)} copy(bf16[8,4,5120]{2,1,0:T(4,128)(2,1)S(1)} %copy-done.3) | data formatting | bytes 655360 | tf_op args[10]
  212.5 12.3 %reshape.302 = bf16[16,2,5120]{2,1,0:T(2,128)(2,1)} reshape(bf16[5120,4,8]{2,1,0:T(4,128)(2,1)} %bitcast.237) | data formatting | bytes 655360
  224.8 14.2 %all-to-all-start.2 = ((bf16[16,2,5120]{2,1,0:T(2,128)(2,1)}), bf16[16,2,5120]{2,1,0:T(2,128)(2,1)S(1)}, u32[]{:S(2)}, u32[]{:S(2)}) async-start(bf16[16,2,5120]{2,1,0:T(2,128)(2,1)} %reshape.302), calls=%async_computation.2 | async-start | bytes 655360 | tf_op jit(solution)/shard_map/all_to_all | solution.py:198
  239.1 1.3 dynamic-slice
  241.0 52.4 %all-reduce.5.cloned.1.call-done = bf16[5120,2,128]{2,1,0:T(2,128)(2,1)} async-done(((bf16[5120,2,128]{2,1,0:T(2,128)(2,1)}), bf16[5120,2,128]{2,1,0:T(2,128)(2,1)}) %all-reduce.5.cloned.1.call-update) | async-done | bytes 2621456
  293.4 2.2 constant_dynamic-slice_fusion.1
  295.6 1.3 dynamic-slice.2
  297.5 91.8 %all-reduce.7.cloned.1.call-done = bf16[1280,2,128]{2,1,0:T(2,128)(2,1)} async-done(((bf16[1280,2,128]{2,1,0:T(2,128)(2,1)}), bf16[1280,2,128]{2,1,0:T(2,128)(2,1)}) %all-reduce.7.cloned.1.call-update) | async-done | bytes 655376
  389.3 1.0 constant_dynamic-slice_fusion
  390.4 1.2 broadcast_in_dim.31
  391.6 5.3 %all-to-all-start.1 = ((f32[4,320,2,128]{3,1,2,0:T(8,128)}), f32[4,320,2,128]{3,1,2,0:T(8,128)S(1)}, u32[]{:S(2)}, u32[]{:S(2)}) async-start(f32[4,320,2,128]{3,1,2,0:T(8,128)} %broadcast_in_dim.31), calls=%async_computation.1 | async-start | bytes 2621440 | tf_op jit(solution)/shard_map/all_to_all | solution.py:30
  396.9 7.2 %reshape.303 = bf16[5120,4,8]{2,1,0:T(4,128)(2,1)} reshape(bf16[16,2,5120]{2,1,0:T(2,128)(2,1)S(1)} %all-to-all-done.2) | data formatting | bytes 655360
  404.1 7.0 %copy.171 = bf16[8,4,16,320]{3,1,0,2:T(4,128)(2,1)S(1)} copy(bf16[8,4,16,320]{0,1,3,2:T(4,128)(2,1)} %bitcast.236) | data formatting | bytes 655360 | tf_op jit(solution)/shard_map/all_to_all | solution.py:198
  411.4 2.6 all-to-all-done.1
  414.9 0.9 reshape_reshape.3
  415.8 6.7 %all-to-all-start.3 = ((f32[16,8,4,256]{3,2,1,0:T(4,128)}), f32[16,8,4,256]{3,2,1,0:T(4,128)S(1)}, u32[]{:S(2)}, u32[]{:S(2)}) async-start(f32[16,8,4,256]{3,2,1,0:T(4,128)} %reshape_reshape.3), calls=%async_computation.3 | async-start | bytes 1048576 | tf_op jit(solution)/shard_map/all_to_all | solution.py:54
  422.6 1.4 copy.229
  424.4 1.0 copy.178
  425.4 1.0 copy.179
  426.4 1.0 copy.180
  427.4 26.3 %all-to-all-done.3 = f32[16,8,4,256]{3,2,1,0:T(4,128)S(1)} async-done(((f32[16,8,4,256]{3,2,1,0:T(4,128)}), f32[16,8,4,256]{3,2,1,0:T(4,128)S(1)}, u32[]{:S(2)}, u32[]{:S(2)}) %all-to-all-start.3) | async-done | bytes 524320 | tf_op jit(solution)/shard_map/all_to_all | solution.py:54
  455.1 0.7 reshape.296
  (55 shorter events, 3.9 us)
Async XLA Ops:
  7.2 114.8 %all-gather.5.cloned.1.call-start = ((), (), s32[]{:S(2)}) async-start(), calls=%async_computation.5 | async-start | bytes 2785280 | tf_op jit(solution)/shard_map/all_gather | solution.py:149
  9.0 179.0 %all-gather.3.cloned.1.call-start = ((), (), s32[]{:S(2)}) async-start(), calls=%async_computation.4 | async-start | bytes 5898240 | tf_op jit(solution)/shard_map/all_gather | solution.py:150
  12.6 37.3 %all-to-all-start = ((f32[64,1,128]{2,1,0:T(1,128)}), f32[64,1,128]{2,1,0:T(1,128)S(1)}, u32[]{:S(2)}, u32[]{:S(2)}) async-start(f32[64,1,128]{2,1,0:T(1,128)} %reshape.300), calls=%async_computation | async-start | bytes 65536 | tf_op jit(solution)/shard_map/all_to_all | solution.py:30
  34.4 259.0 %all-reduce.5.cloned.1.call-start = ((), (), s32[]{:S(2)}) async-start(), calls=%async_computation.6 | async-start | bytes 5242880
  196.7 4.4 slice-start
  198.6 2.5 slice-start.1
  202.8 4.8 %copy-start.3 = (bf16[8,4,5120]{2,1,0:T(4,128)(2,1)S(1)}, bf16[8,4,5120]{2,1,0:T(4,128)(2,1)}, u32[]{:S(2)}) copy-start(bf16[8,4,5120]{2,1,0:T(4,128)(2,1)} %param.24) | copy-start | bytes 983044
  224.8 165.6 %all-to-all-start.2 = ((bf16[16,2,5120]{2,1,0:T(2,128)(2,1)}), bf16[16,2,5120]{2,1,0:T(2,128)(2,1)S(1)}, u32[]{:S(2)}, u32[]{:S(2)}) async-start(bf16[16,2,5120]{2,1,0:T(2,128)(2,1)} %reshape.302), calls=%async_computation.2 | async-start | bytes 655360 | tf_op jit(solution)/shard_map/all_to_all | solution.py:198
  239.0 150.3 %all-reduce.7.cloned.1.call-start = ((), (), s32[]{:S(2)}) async-start(), calls=%async_computation.7 | async-start | bytes 1310720
  391.6 22.3 %all-to-all-start.1 = ((f32[4,320,2,128]{3,1,2,0:T(8,128)}), f32[4,320,2,128]{3,1,2,0:T(8,128)S(1)}, u32[]{:S(2)}, u32[]{:S(2)}) async-start(f32[4,320,2,128]{3,1,2,0:T(8,128)} %broadcast_in_dim.31), calls=%async_computation.1 | async-start | bytes 2621440 | tf_op jit(solution)/shard_map/all_to_all | solution.py:30
  404.1 9.9 %copy-start = (f32[320,2,128]{2,1,0:T(2,128)S(1)}, f32[320,2,128]{2,1,0:T(2,128)}, u32[]{:S(2)}) copy-start(f32[320,2,128]{2,1,0:T(2,128)} %param.21) | copy-start | bytes 983044
  404.1 9.9 %copy-start.1 = (f32[320,2,128]{2,1,0:T(2,128)S(1)}, f32[320,2,128]{2,1,0:T(2,128)}, u32[]{:S(2)}) copy-start(f32[320,2,128]{2,1,0:T(2,128)} %param.22) | copy-start | bytes 983044
  404.1 9.9 %copy-start.2 = (f32[320,2,128]{2,1,0:T(2,128)S(1)}, f32[320,2,128]{2,1,0:T(2,128)}, u32[]{:S(2)}) copy-start(f32[320,2,128]{2,1,0:T(2,128)} %param.23) | copy-start | bytes 983044
  411.1 11.4 %copy-start.4 = (bf16[8,4,640]{2,1,0:T(4,128)(2,1)S(1)}, bf16[8,4,640]{2,1,0:T(4,128)(2,1)}, u32[]{:S(2)}) copy-start(bf16[8,4,640]{2,1,0:T(4,128)(2,1)} %param.25) | copy-start | bytes 122884
  411.3 12.7 %copy-start.5 = (s32[8]{0:T(128)S(1)}, s32[8]{0:T(128)}, u32[]{:S(2)}) copy-start(s32[8]{0:T(128)} %param.27) | copy-start | bytes 100
  415.8 37.9 %all-to-all-start.3 = ((f32[16,8,4,256]{3,2,1,0:T(4,128)}), f32[16,8,4,256]{3,2,1,0:T(4,128)S(1)}, u32[]{:S(2)}, u32[]{:S(2)}) async-start(f32[16,8,4,256]{3,2,1,0:T(4,128)} %reshape_reshape.3), calls=%async_computation.3 | async-start | bytes 1048576 | tf_op jit(solution)/shard_map/all_to_all | solution.py:54
Sparse Core Ops, SparseCore 0:
  11.6 110.3 all-gather.4
  124.1 63.8 all-gather.2
  207.6 85.7 all-reduce.4
  296.2 93.0 all-reduce.6
where the time goes:
time: 463 us; the launch traced here: 462 us
  waiting for transfers between devices  320 us (69%)
  local copies, waits for them, and re-layouts  53.6 us (12%)
  starting transfers between devices  48.1 us (10%)
  between operations  15.4 us (3%)
  matrix products  15.2 us (3%)
  other arithmetic  10.1 us (2%)
    unnamed x6, waiting for transfers between devices  145 us
    all_gather x1, waiting for transfers between devices, body(): weight_full = lax.all_gather(weight_low, FSDP, axis=0, tiled=True)  68.1 us
    all_gather x1, waiting for transfers between devices, body(): tokens_full = lax.all_gather(hidden, 'tensor', axis=1, tiled=True)  66 us
    unnamed x32, local copies, waits for them, and re-layouts  38.2 us
    all_to_all x2, starting transfers between devices, from_everyone(): lax.all_to_all(jnp.broadcast_to(shard[None], (count, *shard.shape)), axis...  27 us
    all_to_all x1, waiting for transfers between devices, summed_on_arrival(): lax.all_to_all(pieces, axis, split_axis=0, concat_axis=0, tiled=True)  26.3 us
    all_to_all x2, waiting for transfers between devices, from_everyone(): lax.all_to_all(jnp.broadcast_to(shard[None], (count, *shard.shape)), axis...  14.4 us
    all_to_all x1, starting transfers between devices, body(): lax.all_to_all(dec_hidden, FSDP, split_axis=2, concat_axis=0, tiled=True)  14.2 us
  transfers between devices with their start and end apart: 8, of which 7 were waited for; matrix products, arithmetic and copies ran while one was open for 11% of the time, Pallas kernels for 0%

commit v1 on v0

v1 whole, which is shorter than its diff:
```python
import functools
import math

import jax
import jax.numpy as jnp
from jax import lax
from jax.experimental import pallas as pl
from jax.experimental.pallas import tpu as pltpu
from jax.sharding import Mesh
from jax.sharding import PartitionSpec as P

D = 5120
QH = 40
KVH = 8
HD = 128
GROUP = 16
RATIO = QH // KVH
AXES = ("x", "zh", "zl", "c", "y")
FSDP = ("x", "zh")
TENSOR = ("zl", "c")
FSDP_POOL = ("x", "zh", "y")
MESH = pl.DeviceIdType.MESH
SEMS = 112

beta_one = 0.9
beta_two = 0.999
learn_rate = 0.001
weight_decay = 0.1
adam_epsilon = 1e-08
adam_step = 10.0
variance_floor = 0.04
masked_score = -1e30
f32 = jnp.float32
bf16 = jnp.bfloat16


def rot(index, step):
    return lax.rem(index + (step + 4), 4)


def remote(src, dst, sends, recvs, k, axis, index):
    return pltpu.make_async_remote_copy(
        src_ref=src,
        dst_ref=dst,
        send_sem=sends.at[k],
        recv_sem=recvs.at[k],
        device_id={axis: index},
        device_id_type=MESH,
    )


class Gather:
    def __init__(self, axis, block, half, sends, recvs, first):
        i = lax.axis_index(axis)
        left, right, far = rot(i, -1), rot(i, 1), rot(i, 2)

        def send(ref, k, index):
            return remote(ref, ref, sends, recvs, first + k, axis, index)

        self.own = (send(block(i), 0, right), send(block(i), 1, left))
        self.near = (send(block(left), 0, right), send(block(right), 1, left))
        self.relay = (send(half(left, 0), 2, right), send(half(right, 1), 3, left))
        self.last = (send(half(far, 0), 2, right), send(half(far, 1), 3, left))

    def start(self):
        for copy in self.own:
            copy.start()

    def forward(self):
        for arrival, copy in zip(self.near, self.relay):
            arrival.wait_recv()
            copy.start()

    def finish(self):
        for arrival in self.last:
            arrival.wait_recv()

    def drain(self):
        for copy in self.own + self.relay:
            copy.wait_send()


class Reduce:
    def __init__(self, axis, half, land, sends, recvs, first):
        i = lax.axis_index(axis)
        left, right, far = rot(i, -1), rot(i, 1), rot(i, 2)
        self.half, self.land = half, land
        self.me, self.left, self.right = i, left, right

        def send(block, h, k, index):
            return remote(half(block, h), land(k), sends, recvs, first + k, axis, index)

        self.copies = (
            send(far, 0, 0, right),
            send(far, 1, 1, left),
            send(right, 1, 2, right),
            send(left, 0, 3, left),
            send(right, 0, 4, right),
            send(left, 1, 5, left),
        )

    def start(self):
        for copy in self.copies[:4]:
            copy.start()

    def forward(self):
        for k, ref in ((0, self.half(self.right, 0)), (1, self.half(self.left, 1))):
            self.copies[k].wait_recv()
            ref[...] = (ref[...].astype(f32) + self.land(k)[...].astype(f32)).astype(bf16)
            self.copies[4 + k].start()

    def finish(self, out):
        for k in (2, 3, 4, 5):
            self.copies[k].wait_recv()
        for h, (one, two) in enumerate(((4, 3), (2, 5))):
            ref = out(h)
            total = self.half(self.me, h)[...].astype(f32) + self.land(one)[...].astype(f32)
            ref[...] = (total + self.land(two)[...].astype(f32)).astype(ref.dtype)

    def drain(self):
        for copy in self.copies:
            copy.wait_send()


class GatherRows:
    def __init__(self, w, sends, recvs, first):
        x, y = lax.axis_index("x"), lax.axis_index("y")
        two = lambda h: pl.ds(2 * h, 2)
        make = lambda axis, block, half, k: Gather(axis, block, half, sends, recvs, first + 4 * k)
        self.deep = make(
            "zh", lambda j: w.at[:, x, j, y], lambda j, h: w.at[h, x, j, y], 0
        )
        self.small = (
            make("x", lambda j: w.at[0, j, :, y], lambda j, h: w.at[0, j, two(h), y], 1),
            make("y", lambda j: w.at[1, x, :, j], lambda j, h: w.at[1, x, two(h), j], 2),
        )
        self.large = (
            make("y", lambda j: w.at[0, :, :, j], lambda j, h: w.at[0, two(h), :, j], 3),
            make("x", lambda j: w.at[1, j], lambda j, h: w.at[1, j, two(h)], 4),
        )

    def drain(self):
        for part in (self.deep,) + self.small + self.large:
            part.drain()


def learner_kernel(
    hidden,
    queries,
    cotangent,
    segment,
    clip,
    rewards,
    order,
    weight,
    moment_one,
    moment_two,
    dec,
    fresh_out,
    grad_out,
    tokens,
    w,
    w_new,
    part,
    acc,
    gacc,
    q_in,
    cot_in,
    m_one,
    m_two,
    dec_in,
    stat,
    stat_land,
    land_k,
    land_v,
    sum_k,
    sum_v,
    land_k_two,
    land_v_two,
    sum_two,
    land_z,
    grads,
    local,
    sends,
    recvs,
):
    x, zh, zl, c, y = (lax.axis_index(name) for name in AXES)
    own_tokens = pltpu.make_async_copy(hidden, tokens.at[zl, c], local.at[0])
    own_tokens.start()
    q_copy = pltpu.make_async_copy(queries, q_in, local.at[1])
    q_copy.start()
    cot_copy = pltpu.make_async_copy(cotangent, cot_in, local.at[2])
    cot_copy.start()
    late = [
        pltpu.make_async_copy(src, dst, local.at[3 + k])
        for k, (src, dst) in enumerate(((moment_one, m_one), (moment_two, m_two), (dec, dec_in)))
    ]
    for copy in late:
        copy.start()

    barrier = pltpu.get_barrier_semaphore()
    peers = [("c", 1 - c)]
    for axis, index in (("zl", zl), ("zh", zh), ("x", x), ("y", y)):
        peers += [(axis, rot(index, d)) for d in (1, 2, 3)]
    for axis, index in peers:
        pl.semaphore_signal(barrier, inc=1, device_id={axis: index}, device_id_type=MESH)

    for h in range(2):
        w[h, x, zh, y] = weight[pl.ds(y * 160 + h, 80, stride=2), :].astype(bf16)
    eye = lax.broadcasted_iota(jnp.int32, (16, 16), 0) == lax.broadcasted_iota(jnp.int32, (16, 16), 1)
    reward_col = jnp.sum(jnp.where(eye, rewards[...], 0.0), axis=1, keepdims=True)
    order_col = jnp.sum(jnp.where(eye, order[...], 0), axis=1, keepdims=True)
    group_col = lax.shift_right_logical(order_col, 4)
    lane = lax.broadcasted_iota(jnp.int32, (16, 128), 1)
    member = lax.bitwise_and(lane, 63) == group_col
    reward_wide = jnp.broadcast_to(reward_col, (16, 128))
    powers = jnp.where(lane < 64, reward_wide, reward_wide * reward_wide)
    stat[0] = jnp.sum(jnp.where(member, powers, 0.0), axis=0, keepdims=True)
    own_tokens.wait()
    pl.semaphore_wait(barrier, len(peers))

    first_stat, first_rows, first_new, first_grads = 0, 9, 29, 49
    first_reduce, first_line = 53, 83
    stat_copies = []
    for k, (axis, index) in enumerate((("zh", zh), ("x", x), ("y", y))):
        stat_copies.append(
            [
                remote(stat.at[k], stat_land.at[k, d - 1], sends, recvs, first_stat + 3 * k + d - 1, axis, rot(index, d))
                for d in (1, 2, 3)
            ]
        )

    def stat_start(k):
        for copy in stat_copies[k]:
            copy.start()

    def stat_finish(k):
        for copy in stat_copies[k]:
            copy.wait_recv()
        stat[k + 1] = ((stat[k] + stat_land[k, 0]) + stat_land[k, 1]) + stat_land[k, 2]

    def shard_right(d):
        ref = tokens.at[zl - d, c]
        return remote(ref, ref, sends, recvs, first_line + d, "zl", zl + 1)

    def shard_left(d):
        ref = tokens.at[zl + d, c]
        return remote(ref, ref, sends, recvs, first_line + 3 + d, "zl", zl - 1)

    def shard_across(j, k):
        ref = tokens.at[j, c]
        return remote(ref, ref, sends, recvs, first_line + 6 + k, "c", 1 - c)

    def arrived(j, k):
        ref = tokens.at[j, c]
        remote(ref, ref, sends, recvs, first_line + k, "c", 1 - c).wait_recv()

    def crossed(j, k):
        ref = tokens.at[j, 1 - c]
        remote(ref, ref, sends, recvs, first_line + 6 + k, "c", 1 - c).wait_recv()

    rows = GatherRows(w, sends, recvs, first_rows)
    rows.deep.start()
    stat_start(0)

    @pl.when(zl < 3)
    def _():
        shard_right(0).start()

    @pl.when(zl > 0)
    def _():
        shard_left(0).start()

    shard_across(zl, 0).start()

    def pass_on(d):
        @pl.when(zl >= d)
        def _():
            arrived(zl - d, d - 1)
            if d < 3:

                @pl.when(zl < 3)
                def _():
                    shard_right(d).start()

            shard_across(zl - d, d).start()

        @pl.when(zl + d <= 3)
        def _():
            arrived(zl + d, 3 + d - 1)
            if d < 3:

                @pl.when(zl > 0)
                def _():
                    shard_left(d).start()

            shard_across(zl + d, 3 + d).start()

    rows.deep.forward()
    rows.deep.finish()
    for part_of in rows.small:
        part_of.start()
    stat_finish(0)
    stat_start(1)
    for part_of in rows.small:
        part_of.forward()
    for part_of in rows.small:
        part_of.finish()
    for part_of in rows.large:
        part_of.start()
    stat_finish(1)
    stat_start(2)
    pass_on(1)
    for part_of in rows.large:
        part_of.forward()
    for part_of in rows.large:
        part_of.finish()
    stat_finish(2)

    def rows_of(source, j, half):
        pieces = [source[h, j, pl.ds(2 * half, 2)].reshape(640, HD) for h in range(2)]
        return jnp.concatenate(pieces, axis=1)

    acc[...] = jnp.zeros_like(acc)

    def project(j):
        for half in range(2):
            acc[...] += jnp.dot(tokens[j, half], rows_of(w, j, half), preferred_element_type=f32)

    crossed(zl, 0)
    project(zl)

    def take(d):
        @pl.when(zl >= d)
        def _():
            crossed(zl - d, d)
            project(zl - d)

        @pl.when(zl + d <= 3)
        def _():
            crossed(zl + d, 3 + d)
            project(zl + d)

    pass_on(2)
    take(1)
    pass_on(3)
    take(2)
    take(3)

    sums = stat[3]
    means = sums[:, :64] / GROUP
    spreads = sums[:, 64:] / GROUP - means * means
    denoms = jnp.sqrt(jnp.maximum(spreads, variance_floor))
    in_group = lax.broadcasted_iota(jnp.int32, (16, 64), 1) == group_col
    mean_col = jnp.sum(jnp.where(in_group, means, 0.0), axis=1, keepdims=True)
    denom_col = jnp.sum(jnp.where(in_group, denoms, 0.0), axis=1, keepdims=True)
    advantage = (reward_col - mean_col) / denom_col
    block = q_in.shape[0]
    seg_row = segment[...]
    of_seq = lax.broadcasted_iota(jnp.int32, (16, block), 0) == seg_row
    coef_row = jnp.sum(jnp.where(of_seq, advantage, 0.0), axis=0, keepdims=True) * clip[...].astype(f32)
    coef_col = jnp.transpose(jnp.broadcast_to(coef_row, (HD, block)))
    seg_float = seg_row.astype(f32)
    seg_col = jnp.transpose(jnp.broadcast_to(seg_float, (HD, block)))

    scale = 1.0 / math.sqrt(HD)
    q_copy.wait()
    cot_copy.wait()
    keys = acc[:, :HD].astype(bf16)
    values = acc[:, HD:].astype(bf16)
    gacc[...] = jnp.zeros_like(gacc)
    contract_last = (((1,), (1,)), ((), ()))
    for i in range(block // HD):
        here = slice(HD * i, HD * (i + 1))
        upto = HD * (i + 1)
        heads = [slice(HD * h, HD * (h + 1)) for h in range(RATIO)]
        q_rows = jnp.concatenate([q_in[here, h] for h in heads], axis=0)
        coef_here = coef_col[here]
        up_rows = jnp.concatenate(
            [(coef_here * cot_in[here, h].astype(f32)).astype(bf16) for h in heads], axis=0
        )
        u_place = lax.broadcasted_iota(jnp.int32, (upto, HD), 0)
        t_place = lax.broadcasted_iota(jnp.int32, (upto, HD), 1) + HD * i
        allowed = (seg_col[:upto] == seg_float[:, here]) & (u_place <= t_place)
        bias = jnp.where(allowed, 0.0, masked_score)
        scores = lax.dot_general(keys[:upto], q_rows, contract_last, preferred_element_type=f32)
        scores = scores * scale + jnp.concatenate([bias] * RATIO, axis=1)
        top = jnp.max(scores, axis=0, keepdims=True)
        weights = jnp.exp(scores - top)
        attention = weights * (1.0 / jnp.sum(weights, axis=0, keepdims=True))
        grad_prob = lax.dot_general(values[:upto], up_rows, contract_last, preferred_element_type=f32)
        inner = jnp.sum(attention * grad_prob, axis=0, keepdims=True)
        grad_score = (attention * (grad_prob - inner) * scale).astype(bf16)
        gacc[:upto, :HD] += jnp.dot(grad_score, q_rows, preferred_element_type=f32)
        gacc[:upto, HD:] += jnp.dot(attention.astype(bf16), up_rows, preferred_element_type=f32)

    grad_kv = gacc[...].astype(bf16)

    def outer(j, carry):
        for half in range(2):
            product = lax.dot_general(
                tokens[j, half], grad_kv, (((0,), (0,)), ((), ())), preferred_element_type=f32
            ).astype(bf16)
            for h in range(2):
                part[h, j, pl.ds(2 * half, 2)] = product[:, HD * h : HD * (h + 1)].reshape(2, 4, 80, HD)
        return carry

    lax.fori_loop(0, 4, outer, 0)

    two = lambda h: pl.ds(2 * h, 2)
    reduce_k = Reduce(
        "y", lambda j, h: part.at[0, two(h), :, j], lambda k: land_k.at[k], sends, recvs, first_reduce
    )
    reduce_v = Reduce(
        "x", lambda j, h: part.at[1, j, two(h)], lambda k: land_v.at[k], sends, recvs, first_reduce + 6
    )
    reduce_k_two = Reduce(
        "x", lambda j, h: sum_k.at[j, two(h)], lambda k: land_k_two.at[k], sends, recvs, first_reduce + 12
    )
    reduce_v_two = Reduce(
        "y", lambda j, h: sum_v.at[two(h), j], lambda k: land_v_two.at[k], sends, recvs, first_reduce + 18
    )
    reduce_z = Reduce(
        "zh", lambda j, h: sum_two.at[h, j], lambda k: land_z.at[k], sends, recvs, first_reduce + 24
    )
    reduce_k.start()
    reduce_v.start()
    reduce_k.forward()
    reduce_v.forward()
    reduce_k.finish(lambda h: sum_k.at[two(h)])
    reduce_k_two.start()
    reduce_v.finish(lambda h: sum_v.at[two(h)])
    reduce_v_two.start()
    reduce_k_two.forward()
    reduce_v_two.forward()
    reduce_k_two.finish(lambda h: sum_two.at[0, two(h)])
    reduce_v_two.finish(lambda h: sum_two.at[1, two(h)])
    reduce_z.start()
    for copy in late:
        copy.wait()
    reduce_z.forward()
    reduce_z.finish(lambda h: grads.at[y, h])

    for h in range(2):
        quarter = pl.ds(y * 160 + h, 80, stride=2)
        grad = grads[y, h]
        one = beta_one * m_one[quarter, :] + (1.0 - beta_one) * grad
        second = beta_two * m_two[quarter, :] + (1.0 - beta_two) * grad * grad
        old = weight[quarter, :]
        new = old - learn_rate * (
            one / (1.0 - beta_one**adam_step) / (jnp.sqrt(second / (1.0 - beta_two**adam_step)) + adam_epsilon)
            + weight_decay * old
        )
        w_new[h, x, zh, y] = new.astype(bf16)
    new_rows = GatherRows(w_new, sends, recvs, first_new)
    new_rows.deep.start()
    all_grads = Gather("y", lambda j: grads.at[j], lambda j, h: grads.at[j, h], sends, recvs, first_grads)
    all_grads.start()
    new_rows.deep.forward()
    new_rows.deep.finish()
    for part_of in new_rows.small:
        part_of.start()
    all_grads.forward()
    for part_of in new_rows.small:
        part_of.forward()
    for part_of in new_rows.small:
        part_of.finish()
    for part_of in new_rows.large:
        part_of.start()
    all_grads.finish()
    grad_out[...] = grads[...]
    for part_of in new_rows.large:
        part_of.forward()
    for part_of in new_rows.large:
        part_of.finish()

    total = jnp.zeros(fresh_out.shape, f32)
    for j in range(4):
        for half in range(2):
            start = 640 * (2 * j + half)
            total += jnp.dot(dec_in[:, start : start + 640], rows_of(w_new, j, half), preferred_element_type=f32)
    fresh_out[...] = total.astype(bf16)

    for group in stat_copies:
        for copy in group:
            copy.wait_send()
    shard_across(zl, 0).wait_send()
    for d in range(3):

        @pl.when((zl >= d) & (zl < 3))
        def _():
            shard_right(d).wait_send()

        @pl.when((zl + d <= 3) & (zl > 0))
        def _():
            shard_left(d).wait_send()

    for d in (1, 2, 3):

        @pl.when(zl >= d)
        def _():
            shard_across(zl - d, d).wait_send()

        @pl.when(zl + d <= 3)
        def _():
            shard_across(zl + d, 3 + d).wait_send()

    for group in (rows, new_rows, all_grads, reduce_k, reduce_v, reduce_k_two, reduce_v_two, reduce_z):
        group.drain()


def learner(hidden, queries, cotangent, segment, clip, rewards, order, weight, moment_one, moment_two, dec):
    anywhere = pl.BlockSpec(memory_space=pl.ANY)
    vmem = pl.BlockSpec(memory_space=pltpu.VMEM)
    block, features = hidden.shape
    full = (2, 4, 4, 4, 80, HD)
    low = lambda *shape: pltpu.VMEM(shape, bf16)
    wide = lambda *shape: pltpu.VMEM(shape, f32)
    return pl.pallas_call(
        learner_kernel,
        out_shape=(
            jax.ShapeDtypeStruct((dec.shape[0], 2 * HD), bf16),
            jax.ShapeDtypeStruct((4, 2, 80, HD), f32),
        ),
        in_specs=[anywhere] * 3 + [vmem] * 5 + [anywhere] * 3,
        out_specs=(vmem, vmem),
        scratch_shapes=[
            low(4, 2, block, features),
            low(*full),
            low(*full),
            low(*full),
            wide(block, 2 * HD),
            wide(block, 2 * HD),
            low(block, features),
            low(block, features),
            wide(640, HD),
            wide(640, HD),
            low(*dec.shape),
            wide(4, 1, HD),
            wide(3, 3, 1, HD),
            low(6, 2, 4, 80, HD),
            low(6, 2, 4, 80, HD),
            low(4, 4, 80, HD),
            low(4, 4, 80, HD),
            low(6, 2, 80, HD),
            low(6, 2, 80, HD),
            low(2, 4, 80, HD),
            low(6, 80, HD),
            wide(4, 2, 80, HD),
            pltpu.SemaphoreType.DMA((6,)),
            pltpu.SemaphoreType.DMA((SEMS,)),
            pltpu.SemaphoreType.DMA((SEMS,)),
        ],
        compiler_params=pltpu.CompilerParams(collective_id=0, has_side_effects=True),
        name="learner",
    )(hidden, queries, cotangent, segment, clip, rewards, order, weight, moment_one, moment_two, dec)


def decode_attend(queries, cache, fresh, lengths):
    head_size = queries.shape[4]
    steps_here = queries.shape[1]
    capacity = cache.shape[1]
    score_scale = 1.0 / math.sqrt(head_size)
    cached = (
        jnp.einsum("bshqd,blhd->bshql", queries, cache[:, :, 0], preferred_element_type=f32)
        * score_scale
    )
    recent = (
        jnp.einsum("bshqd,bjhd->bshqj", queries, fresh[:, :, 0], preferred_element_type=f32)
        * score_scale
    )
    live = jnp.arange(capacity)[None, :] < lengths[:, None]
    cached = jnp.where(live[:, None, None, None, :], cached, masked_score)
    before = jnp.arange(steps_here)[None, :] <= jnp.arange(steps_here)[:, None]
    recent = jnp.where(before[None, :, None, None, :], recent, masked_score)
    row_max = jnp.maximum(
        jnp.max(cached, axis=-1, keepdims=True), jnp.max(recent, axis=-1, keepdims=True)
    )
    cached_exp = jnp.exp(cached - row_max)
    recent_exp = jnp.exp(recent - row_max)
    total = jnp.sum(cached_exp, axis=-1, keepdims=True) + jnp.sum(
        recent_exp, axis=-1, keepdims=True
    )
    cached_low = (cached_exp / total).astype(bf16)
    recent_low = (recent_exp / total).astype(bf16)
    output = jnp.einsum(
        "bshql,blhd->bshqd", cached_low, cache[:, :, 1], preferred_element_type=f32
    )
    output = output + jnp.einsum(
        "bshqj,bjhd->bshqd", recent_low, fresh[:, :, 1], preferred_element_type=f32
    )
    return output.astype(bf16).reshape(queries.shape[0], steps_here, -1)


def body(
    hidden,
    queries,
    cotangent,
    segment,
    clip_mask,
    rewards,
    seq_order,
    kv_weight,
    moment_one,
    moment_two,
    dec_hidden,
    dec_queries,
    kv_cache,
    cache_len,
):
    block_rows = hidden.shape[0]
    fold = lambda value: value.reshape(-1, HD)
    dec_rows, steps_here, _ = dec_hidden.shape
    fresh, grads = learner(
        hidden,
        queries,
        cotangent,
        segment,
        clip_mask.reshape(1, block_rows),
        rewards.reshape(1, -1),
        seq_order.reshape(1, -1),
        fold(kv_weight),
        fold(moment_one),
        fold(moment_two),
        dec_hidden.reshape(dec_rows * steps_here, -1),
    )
    grad = jnp.swapaxes(grads, 1, 2).reshape(kv_weight.shape)
    new_moment_one = beta_one * moment_one + (1.0 - beta_one) * grad
    new_moment_two = beta_two * moment_two + (1.0 - beta_two) * grad * grad
    first_hat = new_moment_one / (1.0 - beta_one**adam_step)
    second_hat = new_moment_two / (1.0 - beta_two**adam_step)
    new_weight = kv_weight - learn_rate * (
        first_hat / (jnp.sqrt(second_hat) + adam_epsilon) + weight_decay * kv_weight
    )
    capacity = kv_cache.shape[1]
    cache = kv_cache.reshape(dec_rows, capacity, 2, 1, HD)
    query_dec = dec_queries.reshape(dec_rows, steps_here, 1, RATIO, HD)
    fresh_low = fresh.reshape(dec_rows, steps_here, 2, 1, HD)
    dec_out = decode_attend(query_dec, cache, fresh_low, cache_len)
    return (new_weight, new_moment_one, new_moment_two, dec_out)


def solution(mesh):
    finer = Mesh(mesh.devices.reshape(4, 4, 4, 2, 4), AXES)
    in_specs = (
        P(FSDP_POOL, TENSOR),
        P(FSDP_POOL, TENSOR),
        P(FSDP_POOL, TENSOR),
        P(FSDP_POOL, None),
        P(FSDP_POOL),
        P(FSDP_POOL),
        P(FSDP_POOL),
        P(FSDP, None, TENSOR),
        P(FSDP, None, TENSOR),
        P(FSDP, None, TENSOR),
        P(FSDP_POOL, None, None),
        P(FSDP_POOL, None, TENSOR),
        P(FSDP_POOL, None, None, TENSOR),
        P(FSDP_POOL),
    )
    out_specs = (
        P(FSDP, None, TENSOR),
        P(FSDP, None, TENSOR),
        P(FSDP, None, TENSOR),
        P(FSDP_POOL, None, TENSOR),
    )
    return jax.shard_map(body, mesh=finer, in_specs=in_specs, out_specs=out_specs, check_vma=False)
```

time: 463 us -> 159 us (0.34)
  the two profiles are of different devices: /device:TPU:1 before, /device:TPU:16 now
where the time goes in v1:
time: 159 us; the launch traced here: 158 us
  Pallas kernels  147 us (92%)
  local copies, waits for them, and re-layouts  8.86 us (6%)
    pallas_call x1, Pallas kernels, learner(): pl.pallas_call(learner_kernel, out_shape=(jax.ShapeDtypeStruct((dec.shape...  147 us
    unnamed x18, local copies, waits for them, and re-layouts  5.62 us

profile of v1, /device:TPU:16, one launch (start us, length us, event | category | flops | bytes accessed | tf_op | source)
XLA Modules:
  0.0 158.5 jit_solution(11020109901143151276)
XLA Ops:
  0.6 1.8 %reshape.153.dec = bf16[32,5120]{1,0:T(8,128)(2,1)} reshape(bf16[8,4,5120]{2,1,0:T(4,128)(2,1)} %param.24) | data formatting | bytes 655360 | tf_op jit(solution)/shard_map/reshape | solution.py:625
  2.4 0.0 copy-start.3
  2.4 147.0 %learner.1 = (bf16[32,256]{1,0:T(8,128)(2,1)}, f32[4,2,80,128]{3,2,1,0:T(8,128)}) custom-call(bf16[512,640]{1,0:T(8,128)(2,1)} %hidden.1, bf16[512,640]{1,0:T(8,128)(2,1)} %queries.1, bf16[512,640]{1,0:T(8,128)(2,1)} %cotangent.1, s32[1,512]{1,0:T(1,128)} %segment.1, s32[1,512]{1,0:T(1,128)} %bitcast.91, f32[1,16]{1,0:T(1,128)} %bitcast.92, ...), custom_call_target="tpu_custom_call" | custom-call | tf_op jit(solution)/shard_map/learner/pallas_call | solution.py:519
  149.4 0.7 reshape.158
  150.1 0.0 copy-start.5
  150.1 0.7 copy-done.5
  150.9 0.4 fusion.21
  151.3 0.0 copy-done.3
  151.4 0.2 copy.61
  151.6 0.0 copy-start.6
  151.6 0.6 copy-done.6
  152.2 0.1 iota_compare_fusion
  152.3 0.4 fusion.20
  152.7 0.1 fusion.13
  152.7 0.2 fusion.10
  153.0 0.2 fusion.14
  153.2 0.0 copy-start.4
  153.2 0.0 copy-start.2
  153.2 0.3 fusion.5
  153.5 0.7 reshape.169
  154.2 0.0 copy-done.4
  154.2 0.0 copy-start
  154.2 0.0 copy-start.1
  154.2 0.1 copy-done.2
  154.3 0.9 copy-done
  155.2 0.1 copy-done.1
  155.3 0.3 multiply_subtract_fusion
  155.6 1.0 copy.33
  156.5 1.0 copy.34
  157.5 1.0 copy.35
  (6 shorter events, 0.1 us)
Async XLA Ops:
  2.4 148.9 %copy-start.3 = (bf16[8,256,2,128]{3,2,1,0:T(2,128)(2,1)S(1)}, bf16[8,256,2,128]{3,2,1,0:T(2,128)(2,1)}, u32[]{:S(2)}) copy-start(bf16[8,256,2,128]{3,2,1,0:T(2,128)(2,1)} %param.26) | copy-start | bytes 3145732
  150.1 0.8 copy-start.5
  151.6 0.7 copy-start.6
  153.2 1.0 copy-start.4
  153.2 1.1 copy-start.2
  154.2 1.0 copy-start
  154.2 1.1 copy-start.1

commit v2 on v1

v2 whole, which is shorter than its diff:
```python
import functools
import math

import jax
import jax.numpy as jnp
from jax import lax
from jax.experimental import pallas as pl
from jax.experimental.pallas import tpu as pltpu
from jax.sharding import Mesh
from jax.sharding import PartitionSpec as P

D = 5120
QH = 40
KVH = 8
HD = 128
GROUP = 16
RATIO = QH // KVH
AXES = ("x", "zh", "zl", "c", "y")
FSDP = ("x", "zh")
TENSOR = ("zl", "c")
FSDP_POOL = ("x", "zh", "y")
MESH = pl.DeviceIdType.MESH
SEMS = 232

beta_one = 0.9
beta_two = 0.999
learn_rate = 0.001
weight_decay = 0.1
adam_epsilon = 1e-08
adam_step = 10.0
variance_floor = 0.04
masked_score = -1e30
f32 = jnp.float32
bf16 = jnp.bfloat16


def rot(index, step):
    return lax.rem(index + (step + 4), 4)


def remote(src, dst, sends, recvs, k, axis, index):
    return pltpu.make_async_remote_copy(
        src_ref=src,
        dst_ref=dst,
        send_sem=sends.at[k],
        recv_sem=recvs.at[k],
        device_id={axis: index},
        device_id_type=MESH,
    )


class Gather:
    def __init__(self, axis, block, half, sends, recvs, spot):
        i = lax.axis_index(axis)
        left, right, far = rot(i, -1), rot(i, 1), rot(i, 2)
        first = spot.take(6)

        def send(ref, k, index):
            return remote(ref, ref, sends, recvs, first + k, axis, index)

        def arrival(ref, k):
            return send(ref, k, right)

        self.own = (
            send(half(i, 0), 0, right),
            send(half(i, 1), 1, left),
            send(half(i, 1), 2, right),
            send(half(i, 0), 3, left),
        )
        self.first_half = (arrival(half(left, 0), 0), arrival(half(right, 1), 1))
        self.second_half = (arrival(half(left, 1), 2), arrival(half(right, 0), 3))
        self.relay = (send(half(left, 0), 4, right), send(half(right, 1), 5, left))
        self.from_far = (arrival(half(far, 0), 4), arrival(half(far, 1), 5))

    def start(self):
        for copy in self.own:
            copy.start()

    def forward(self):
        for got, copy in zip(self.first_half, self.relay):
            got.wait_recv()
            copy.start()

    def near(self):
        for got in self.second_half:
            got.wait_recv()

    def last(self):
        for got in self.from_far:
            got.wait_recv()

    def finish(self):
        self.near()
        self.last()

    def drain(self):
        for copy in self.own + self.relay:
            copy.wait_send()


class DirectGather:
    def __init__(self, axis, block, sends, recvs, spot):
        i = lax.axis_index(axis)
        first = spot.take(3)
        self.own = [remote(block(i), block(i), sends, recvs, first + d - 1, axis, rot(i, d)) for d in (2, 1, 3)]
        self.others = [
            remote(block(rot(i, -d)), block(rot(i, -d)), sends, recvs, first + d - 1, axis, rot(i, d))
            for d in (1, 3, 2)
        ]

    def start(self):
        for copy in self.own:
            copy.start()

    def finish(self):
        for got in self.others:
            got.wait_recv()

    def drain(self):
        for copy in self.own:
            copy.wait_send()


class DirectReduce:
    def __init__(self, axis, block, land, sends, recvs, spot):
        i = lax.axis_index(axis)
        first = spot.take(3)
        self.mine, self.land = block(i), land
        self.copies = [
            remote(block(rot(i, d)), land(d - 1), sends, recvs, first + d - 1, axis, rot(i, d)) for d in (2, 1, 3)
        ]

    def start(self):
        for copy in self.copies:
            copy.start()

    def finish(self, out):
        for copy in self.copies:
            copy.wait_recv()
        total = self.mine[...].astype(f32)
        for k in range(3):
            total = total + self.land(k)[...].astype(f32)
        out[...] = total.astype(out.dtype)

    def drain(self):
        for copy in self.copies:
            copy.wait_send()


class Spots:
    def __init__(self):
        self.free = 0

    def take(self, count):
        first = self.free
        self.free += count
        return first


class Reduce:
    def __init__(self, axis, half, land, sends, recvs, spot):
        i = lax.axis_index(axis)
        first = spot.take(6)
        left, right, far = rot(i, -1), rot(i, 1), rot(i, 2)
        self.half, self.land = half, land
        self.me, self.left, self.right = i, left, right

        def send(block, h, k, index):
            return remote(half(block, h), land(k, h), sends, recvs, first + k, axis, index)

        self.copies = (
            send(far, 0, 0, right),
            send(far, 1, 1, left),
            send(right, 1, 2, right),
            send(left, 0, 3, left),
            send(right, 0, 4, right),
            send(left, 1, 5, left),
        )

    def start_far(self):
        for copy in self.copies[:2]:
            copy.start()

    def start_near(self):
        for copy in self.copies[2:4]:
            copy.start()

    def start(self):
        self.start_far()
        self.start_near()

    def forward(self):
        for h, ref in ((0, self.half(self.right, 0)), (1, self.half(self.left, 1))):
            self.copies[h].wait_recv()
            ref[...] = (ref[...].astype(f32) + self.land(h, h)[...].astype(f32)).astype(bf16)
            self.copies[4 + h].start()

    def finish(self, out):
        for k in (2, 3, 4, 5):
            self.copies[k].wait_recv()
        for h, (one, two) in enumerate(((4, 3), (2, 5))):
            ref = out(h)
            total = self.half(self.me, h)[...].astype(f32) + self.land(one, h)[...].astype(f32)
            ref[...] = (total + self.land(two, h)[...].astype(f32)).astype(ref.dtype)

    def drain(self):
        for copy in self.copies:
            copy.wait_send()


def pair(h):
    return pl.ds(2 * h, 2)


class Both:
    def __init__(self, *parts):
        self.parts = parts

    def __getattr__(self, name):
        def run(*given):
            for k, part in enumerate(self.parts):
                getattr(part, name)(*(value[k] for value in given))

        return run


class GatherRows:
    def __init__(self, w, pieces, sends, recvs, spot):
        x, y = lax.axis_index("x"), lax.axis_index("y")
        ring = lambda axis, block, half: Gather(axis, block, half, sends, recvs, spot)
        direct = lambda axis, block: DirectGather(axis, block, sends, recvs, spot)
        self.deep = ring("zh", lambda j: w.at[:, x, j, y], lambda j, h: w.at[h, x, j, y])
        self.small, self.large = [], []
        for p in pieces:
            self.small.append(
                Both(direct("x", lambda i: w.at[0, i, p, y]), direct("y", lambda i: w.at[1, x, p, i]))
            )
            self.large.append(
                Both(
                    ring("y", lambda i: w.at[0, :, p, i], lambda i, h: w.at[0, pair(h), p, i]),
                    ring("x", lambda i: w.at[1, i, p], lambda i, h: w.at[1, i, p, pair(h)]),
                )
            )

    def drain(self):
        for part in [self.deep] + self.small + self.large:
            part.drain()


def learner_kernel(
    hidden,
    queries,
    cotangent,
    segment,
    clip,
    rewards,
    order,
    weight,
    moment_one,
    moment_two,
    dec,
    dec_queries,
    kv_cache,
    cache_len,
    weight_out,
    one_out,
    two_out,
    dec_out,
    tokens,
    w,
    w_new,
    part,
    acc,
    gacc,
    q_in,
    cot_in,
    m_one,
    m_two,
    dec_in,
    dec_wide,
    dec_cut,
    cache_in,
    dec_q,
    cached,
    top_sum,
    stat,
    stat_land,
    land_k,
    land_v,
    sum_k,
    sum_v,
    land_k_two,
    land_v_two,
    sum_two,
    land_z,
    grads,
    local,
    sends,
    recvs,
):
    x, zh, zl, c, y = (lax.axis_index(name) for name in AXES)
    own_tokens = pltpu.make_async_copy(hidden, tokens.at[zl, c], local.at[0])
    own_tokens.start()
    q_copy = pltpu.make_async_copy(queries, q_in, local.at[1])
    q_copy.start()
    cot_copy = pltpu.make_async_copy(cotangent, cot_in, local.at[2])
    cot_copy.start()
    late = [
        pltpu.make_async_copy(src, dst, local.at[3 + k])
        for k, (src, dst) in enumerate(
            ((moment_one, m_one), (moment_two, m_two), (dec, dec_in), (kv_cache, cache_in))
        )
    ]
    for copy in late:
        copy.start()

    barrier = pltpu.get_barrier_semaphore()
    peers = [("c", 1 - c)]
    for axis, index in (("zl", zl), ("zh", zh), ("x", x), ("y", y)):
        peers += [(axis, rot(index, d)) for d in ((1, -1, 2) if axis in ("x", "y") else (1, -1))]
    for axis, index in peers:
        pl.semaphore_signal(barrier, inc=1, device_id={axis: index}, device_id_type=MESH)

    for h in range(2):
        w[h, x, zh, y] = weight[pl.ds(y * 160 + h, 80, stride=2), :].astype(bf16)
    eye = lax.broadcasted_iota(jnp.int32, (16, 16), 0) == lax.broadcasted_iota(jnp.int32, (16, 16), 1)
    reward_col = jnp.sum(jnp.where(eye, rewards[...], 0.0), axis=1, keepdims=True)
    order_col = jnp.sum(jnp.where(eye, order[...], 0), axis=1, keepdims=True)
    group_col = lax.shift_right_logical(order_col, 4)
    lane = lax.broadcasted_iota(jnp.int32, (16, 128), 1)
    member = lax.bitwise_and(lane, 63) == group_col
    reward_wide = jnp.broadcast_to(reward_col, (16, 128))
    powers = jnp.where(lane < 64, reward_wide, reward_wide * reward_wide)
    stat[0] = jnp.sum(jnp.where(member, powers, 0.0), axis=0, keepdims=True)
    own_tokens.wait()
    pl.semaphore_wait(barrier, len(peers))

    spot = Spots()
    first_stat, first_line = spot.take(9), spot.take(13)
    stat_copies = []
    for k, (axis, index) in enumerate((("zh", zh), ("x", x), ("y", y))):
        stat_copies.append(
            [
                remote(src, stat_land.at[k, n], sends, recvs, first_stat + 3 * k + n, axis, rot(index, d))
                for n, (src, d) in enumerate(((stat.at[k], 1), (stat.at[k], -1), (stat_land.at[k, 0], 1)))
            ]
        )

    def stat_start(k):
        for copy in stat_copies[k][:2]:
            copy.start()

    def stat_forward(k):
        stat_copies[k][0].wait_recv()
        stat_copies[k][2].start()

    def stat_finish(k):
        for copy in stat_copies[k][1:]:
            copy.wait_recv()
        stat[k + 1] = (stat[k] + stat_land[k, 0]) + (stat_land[k, 1] + stat_land[k, 2])

    def shard_right(d):
        ref = tokens.at[zl - d, c]
        return remote(ref, ref, sends, recvs, first_line + d, "zl", zl + 1)

    def shard_left(d):
        ref = tokens.at[zl + d, c]
        return remote(ref, ref, sends, recvs, first_line + 3 + d, "zl", zl - 1)

    def shard_across(j, k):
        ref = tokens.at[j, c]
        return remote(ref, ref, sends, recvs, first_line + 6 + k, "c", 1 - c)

    def arrived(j, k):
        ref = tokens.at[j, c]
        remote(ref, ref, sends, recvs, first_line + k, "c", 1 - c).wait_recv()

    def crossed(j, k):
        ref = tokens.at[j, 1 - c]
        remote(ref, ref, sends, recvs, first_line + 6 + k, "c", 1 - c).wait_recv()

    whole = pl.ds(0, 4)
    rows = GatherRows(w, (whole,), sends, recvs, spot)
    rows.deep.start()
    stat_start(0)

    @pl.when(zl < 3)
    def _():
        shard_right(0).start()

    @pl.when(zl > 0)
    def _():
        shard_left(0).start()

    shard_across(zl, 0).start()

    def pass_on(d):
        @pl.when(zl >= d)
        def _():
            arrived(zl - d, d - 1)
            if d < 3:

                @pl.when(zl < 3)
                def _():
                    shard_right(d).start()

            shard_across(zl - d, d).start()

        @pl.when(zl + d <= 3)
        def _():
            arrived(zl + d, 3 + d - 1)
            if d < 3:

                @pl.when(zl > 0)
                def _():
                    shard_left(d).start()

            shard_across(zl + d, 3 + d).start()

    rows.deep.forward()
    stat_forward(0)
    rows.deep.finish()
    rows.small[0].start()
    stat_finish(0)
    stat_start(1)
    stat_forward(1)
    rows.small[0].finish()
    rows.large[0].start()
    stat_finish(1)
    stat_start(2)
    pass_on(1)
    rows.large[0].forward()
    stat_forward(2)
    rows.large[0].finish()
    stat_finish(2)

    def rows_of(source, j, half):
        pieces = [source[h, j, pl.ds(2 * half, 2)].reshape(640, HD) for h in range(2)]
        return jnp.concatenate(pieces, axis=1)

    acc[...] = jnp.zeros_like(acc)

    def project(j):
        for half in range(2):
            acc[...] += jnp.dot(tokens[j, half], rows_of(w, j, half), preferred_element_type=f32)

    crossed(zl, 0)
    project(zl)

    def take(d):
        @pl.when(zl >= d)
        def _():
            crossed(zl - d, d)
            project(zl - d)

        @pl.when(zl + d <= 3)
        def _():
            crossed(zl + d, 3 + d)
            project(zl + d)

    pass_on(2)
    take(1)

    for copy in late:
        copy.wait()
    requests, steps, _ = dec_q.shape[0] // (8 * RATIO), dec_in.shape[1], None
    wide_rows = 8 * RATIO
    scale = 1.0 / math.sqrt(HD)
    contract_last = (((1,), (1,)), ((), ()))
    dec_q[...] = jnp.zeros_like(dec_q)
    for r in range(requests):
        dec_wide[steps * r : steps * (r + 1), :] = dec_in[r].astype(f32)
        for h in range(RATIO):
            start = wide_rows * r + 8 * h
            dec_q[start : start + steps, :] = dec_queries[r, :, HD * h : HD * (h + 1)].astype(f32)
    for f in range(16):
        dec_cut[f] = dec_wide[:, 320 * f : 320 * (f + 1)].astype(bf16)
    place = lax.broadcasted_iota(jnp.int32, (wide_rows, cache_in.shape[1]), 1)
    for r in range(requests):
        mine = slice(wide_rows * r, wide_rows * (r + 1))
        dots = lax.dot_general(dec_q[mine, :].astype(bf16), cache_in[r], contract_last, preferred_element_type=f32)
        live = (place < 2 * cache_len[r]) & (lax.bitwise_and(place, 1) == 0)
        dots = jnp.where(live, dots * scale, masked_score)
        top = jnp.max(dots, axis=1, keepdims=True)
        powers = jnp.exp(dots - top)
        top_sum[0, mine, :] = jnp.broadcast_to(top, (wide_rows, HD))
        top_sum[1, mine, :] = jnp.broadcast_to(jnp.sum(powers, axis=1, keepdims=True), (wide_rows, HD))
        cached[r] = pltpu.roll(powers, 1, 1)

    pass_on(3)
    take(2)
    take(3)

    sums = stat[3]
    means = sums[:, :64] / GROUP
    spreads = sums[:, 64:] / GROUP - means * means
    denoms = jnp.sqrt(jnp.maximum(spreads, variance_floor))
    in_group = lax.broadcasted_iota(jnp.int32, (16, 64), 1) == group_col
    mean_col = jnp.sum(jnp.where(in_group, means, 0.0), axis=1, keepdims=True)
    denom_col = jnp.sum(jnp.where(in_group, denoms, 0.0), axis=1, keepdims=True)
    advantage = (reward_col - mean_col) / denom_col
    block = q_in.shape[0]
    seg_row = segment[...]
    of_seq = lax.broadcasted_iota(jnp.int32, (16, block), 0) == seg_row
    coef_row = jnp.sum(jnp.where(of_seq, advantage, 0.0), axis=0, keepdims=True) * clip[...].astype(f32)
    coef_col = jnp.transpose(jnp.broadcast_to(coef_row, (HD, block)))
    seg_float = seg_row.astype(f32)
    seg_col = jnp.transpose(jnp.broadcast_to(seg_float, (HD, block)))

    q_copy.wait()
    cot_copy.wait()
    keys = acc[:, :HD].astype(bf16)
    values = acc[:, HD:].astype(bf16)
    gacc[...] = jnp.zeros_like(gacc)
    for i in range(block // HD):
        here = slice(HD * i, HD * (i + 1))
        upto = HD * (i + 1)
        heads = [slice(HD * h, HD * (h + 1)) for h in range(RATIO)]
        q_rows = jnp.concatenate([q_in[here, h] for h in heads], axis=0)
        coef_here = coef_col[here]
        up_rows = jnp.concatenate(
            [(coef_here * cot_in[here, h].astype(f32)).astype(bf16) for h in heads], axis=0
        )
        u_place = lax.broadcasted_iota(jnp.int32, (upto, HD), 0)
        t_place = lax.broadcasted_iota(jnp.int32, (upto, HD), 1) + HD * i
        allowed = (seg_col[:upto] == seg_float[:, here]) & (u_place <= t_place)
        bias = jnp.where(allowed, 0.0, masked_score)
        scores = lax.dot_general(keys[:upto], q_rows, contract_last, preferred_element_type=f32)
        scores = scores * scale + jnp.concatenate([bias] * RATIO, axis=1)
        top = jnp.max(scores, axis=0, keepdims=True)
        weights = jnp.exp(scores - top)
        attention = weights * (1.0 / jnp.sum(weights, axis=0, keepdims=True))
        grad_prob = lax.dot_general(values[:upto], up_rows, contract_last, preferred_element_type=f32)
        inner = jnp.sum(attention * grad_prob, axis=0, keepdims=True)
        grad_score = (attention * (grad_prob - inner) * scale).astype(bf16)
        gacc[:upto, :HD] += jnp.dot(grad_score, q_rows, preferred_element_type=f32)
        gacc[:upto, HD:] += jnp.dot(attention.astype(bf16), up_rows, preferred_element_type=f32)

    grad_kv = gacc[...].astype(bf16)

    def outer(half):
        def step(j, carry):
            product = lax.dot_general(
                tokens[j, half], grad_kv, (((0,), (0,)), ((), ())), preferred_element_type=f32
            ).astype(bf16)
            for h in range(2):
                part[h, j, pl.ds(2 * half, 2)] = product[:, HD * h : HD * (h + 1)].reshape(2, 4, 80, HD)
            return carry

        lax.fori_loop(0, 4, step, 0)

    far = rot(zh, 2)
    near = lambda p: p + 1 - 2 * lax.rem(p, 2)
    order_of = (far, near(far), near(zh), zh)
    ring = lambda axis, half, land: Reduce(axis, half, land, sends, recvs, spot)
    direct = lambda axis, block, land: DirectReduce(axis, block, land, sends, recvs, spot)
    one, two, one_to, two_to = [], [], [], []
    for n, p in enumerate(order_of):
        one.append(
            Both(
                ring("y", lambda i, h, p=p: part.at[0, pair(h), p, i], lambda k, h, n=n: land_k.at[n, k]),
                ring("x", lambda i, h, p=p: part.at[1, i, p, pair(h)], lambda k, h, n=n: land_v.at[n, k]),
            )
        )
        one_to.append((lambda h, p=p: sum_k.at[pair(h), p], lambda h, p=p: sum_v.at[p, pair(h)]))
        two.append(
            Both(
                direct("x", lambda i, p=p: sum_k.at[i, p], lambda k, n=n: land_k_two.at[n, k]),
                direct("y", lambda i, p=p: sum_v.at[p, i], lambda k, n=n: land_v_two.at[n, k]),
            )
        )
        two_to.append((sum_two.at[0, p], sum_two.at[1, p]))
    reduce_z = ring("zh", lambda j, h: sum_two.at[h, j], lambda k, h: land_z.at[k])

    outer(lax.div(far, 2))
    one[0].start()
    outer(lax.div(zh, 2))
    one[1].start()
    one[0].forward()
    one[2].start()
    one[0].finish(one_to[0])
    two[0].start()
    one[1].forward()
    one[3].start()
    one[1].finish(one_to[1])
    two[1].start()
    two[0].finish(two_to[0])
    reduce_z.start_far()
    one[2].forward()
    one[2].finish(one_to[2])
    two[2].start()
    one[3].forward()
    two[1].finish(two_to[1])
    two[2].finish(two_to[2])
    reduce_z.start_near()
    one[3].finish(one_to[3])
    two[3].start()
    reduce_z.forward()
    two[3].finish(two_to[3])
    reduce_z.finish(lambda h: grads.at[y, h])

    def update(start, h, grad):
        rows_here = pl.ds(start + h, 80, stride=2)
        first = beta_one * m_one[rows_here, :] + (1.0 - beta_one) * grad
        second = beta_two * m_two[rows_here, :] + (1.0 - beta_two) * grad * grad
        old = weight[rows_here, :]
        first_hat = first / (1.0 - beta_one**adam_step)
        second_hat = second / (1.0 - beta_two**adam_step)
        new = old - learn_rate * (first_hat / (jnp.sqrt(second_hat) + adam_epsilon) + weight_decay * old)
        return rows_here, new, first, second

    for h in range(2):
        w_new[h, x, zh, y] = update(y * 160, h, grads[y, h])[1].astype(bf16)
    pieces = (zh, rot(zh, -1), rot(zh, 1), far)
    new_rows = GatherRows(w_new, pieces, sends, recvs, spot)
    small, large = new_rows.small, new_rows.large
    all_grads = Gather("y", lambda j: grads.at[j], lambda j, h: grads.at[j, h], sends, recvs, spot)
    fresh_total = jnp.zeros((dec_wide.shape[0], 2 * HD), f32)

    def fresh_of(p):
        added = jnp.zeros((dec_wide.shape[0], 2 * HD), f32)
        for i in range(4):
            columns = jnp.concatenate([w_new[h, i, p].reshape(320, HD) for h in range(2)], axis=1)
            added += jnp.dot(dec_cut[4 * i + p], columns, preferred_element_type=f32)
        return added

    new_rows.deep.start()
    small[0].start()
    all_grads.start()
    small[0].finish()
    large[0].start()
    all_grads.forward()
    new_rows.deep.forward()
    new_rows.deep.near()
    small[1].start()
    small[2].start()
    large[0].forward()
    small[1].finish()
    large[1].start()
    small[2].finish()
    large[2].start()
    new_rows.deep.last()
    small[3].start()
    large[0].finish()
    large[1].forward()
    small[3].finish()
    large[3].start()
    large[2].forward()
    fresh_total += fresh_of(pieces[0])
    large[1].finish()
    fresh_total += fresh_of(pieces[1])
    large[3].forward()
    large[2].finish()
    fresh_total += fresh_of(pieces[2])
    large[3].finish()
    fresh_total += fresh_of(pieces[3])

    fresh = fresh_total.astype(bf16)
    recent = lax.dot_general(dec_q[...].astype(bf16), fresh[:, :HD], contract_last, preferred_element_type=f32)
    row = lax.broadcasted_iota(jnp.int32, recent.shape, 0)
    column = lax.broadcasted_iota(jnp.int32, recent.shape, 1)
    first_row = lax.div(column, steps) * wide_rows
    seen = (row >= first_row) & (row < first_row + wide_rows)
    seen = seen & (lax.rem(column, steps) <= lax.bitwise_and(row, 7))
    recent = jnp.where(seen, recent * scale, masked_score)
    old_top = top_sum[0, :, :1]
    top = jnp.maximum(old_top, jnp.max(recent, axis=1, keepdims=True))
    shrink = jnp.exp(old_top - top)
    powers = jnp.exp(recent - top)
    total = top_sum[1, :, :1] * shrink + jnp.sum(powers, axis=1, keepdims=True)
    by_fresh = jnp.dot((powers / total).astype(bf16), fresh[:, HD:], preferred_element_type=f32)
    factor = shrink / total
    for r in range(requests):
        mine = slice(wide_rows * r, wide_rows * (r + 1))
        dec_weights = (cached[r] * factor[mine]).astype(bf16)
        result = by_fresh[mine] + jnp.dot(dec_weights, cache_in[r], preferred_element_type=f32)
        for h in range(RATIO):
            dec_out[r, :, HD * h : HD * (h + 1)] = result[8 * h : 8 * h + steps].astype(bf16)

    all_grads.finish()
    for quarter in range(4):
        for h in range(2):
            rows_here, new, first, second = update(160 * quarter, h, grads[quarter, h])
            weight_out[rows_here, :] = new
            one_out[rows_here, :] = first
            two_out[rows_here, :] = second

    for group in stat_copies:
        for copy in group:
            copy.wait_send()
    shard_across(zl, 0).wait_send()
    for d in range(3):

        @pl.when((zl >= d) & (zl < 3))
        def _():
            shard_right(d).wait_send()

        @pl.when((zl + d <= 3) & (zl > 0))
        def _():
            shard_left(d).wait_send()

    for d in (1, 2, 3):

        @pl.when(zl >= d)
        def _():
            shard_across(zl - d, d).wait_send()

        @pl.when(zl + d <= 3)
        def _():
            shard_across(zl + d, 3 + d).wait_send()

    for group in [rows, new_rows, all_grads, reduce_z] + one + two:
        group.drain()


def learner(*operands):
    hidden, dec, dec_queries, kv_cache = operands[0], operands[10], operands[11], operands[12]
    anywhere = pl.BlockSpec(memory_space=pl.ANY)
    vmem = pl.BlockSpec(memory_space=pltpu.VMEM)
    block, features = hidden.shape
    requests = dec.shape[0]
    full = (2, 4, 4, 4, 80, HD)
    low = lambda *shape: pltpu.VMEM(shape, bf16)
    wide = lambda *shape: pltpu.VMEM(shape, f32)
    return pl.pallas_call(
        learner_kernel,
        out_shape=(
            jax.ShapeDtypeStruct((640, HD), f32),
            jax.ShapeDtypeStruct((640, HD), f32),
            jax.ShapeDtypeStruct((640, HD), f32),
            jax.ShapeDtypeStruct(dec_queries.shape, bf16),
        ),
        in_specs=[anywhere] * 3 + [vmem] * 5 + [anywhere] * 3 + [vmem, anywhere, pl.BlockSpec(memory_space=pltpu.SMEM)],
        out_specs=(vmem,) * 4,
        scratch_shapes=[
            low(4, 2, block, features),
            low(*full),
            low(*full),
            low(*full),
            wide(block, 2 * HD),
            wide(block, 2 * HD),
            low(block, features),
            low(block, features),
            wide(640, HD),
            wide(640, HD),
            low(*dec.shape),
            wide(requests * dec.shape[1], dec.shape[2]),
            low(16, requests * dec.shape[1], 320),
            low(*kv_cache.shape),
            wide(requests * 8 * RATIO, HD),
            wide(requests, 8 * RATIO, kv_cache.shape[1]),
            wide(2, requests * 8 * RATIO, HD),
            wide(4, 1, HD),
            wide(3, 3, 1, HD),
            low(4, 6, 2, 80, HD),
            low(4, 6, 2, 80, HD),
            low(4, 4, 80, HD),
            low(4, 4, 80, HD),
            low(4, 3, 80, HD),
            low(4, 3, 80, HD),
            low(2, 4, 80, HD),
            low(6, 80, HD),
            wide(4, 2, 80, HD),
            pltpu.SemaphoreType.DMA((7,)),
            pltpu.SemaphoreType.DMA((SEMS,)),
            pltpu.SemaphoreType.DMA((SEMS,)),
        ],
        compiler_params=pltpu.CompilerParams(collective_id=0, has_side_effects=True),
        name="learner",
    )(*operands)


def put_kernel(*refs):
    count = (len(refs) - 1) // 2
    copies = [pltpu.make_async_copy(refs[k], refs[count + k], refs[-1].at[k]) for k in range(count)]
    for copy in copies:
        copy.start()
    for copy in copies:
        copy.wait()


def put(*arrays):
    return pl.pallas_call(
        put_kernel,
        out_shape=[jax.ShapeDtypeStruct(array.shape, array.dtype) for array in arrays],
        in_specs=[pl.BlockSpec(memory_space=pltpu.VMEM)] * len(arrays),
        out_specs=[pl.BlockSpec(memory_space=pltpu.HBM)] * len(arrays),
        scratch_shapes=[pltpu.SemaphoreType.DMA((len(arrays),))],
        name="put",
    )(*arrays)


def body(
    hidden,
    queries,
    cotangent,
    segment,
    clip_mask,
    rewards,
    seq_order,
    kv_weight,
    moment_one,
    moment_two,
    dec_hidden,
    dec_queries,
    kv_cache,
    cache_len,
):
    block_rows = hidden.shape[0]
    fold = lambda value: value.reshape(-1, HD)
    requests, capacity = kv_cache.shape[:2]
    results = learner(
        hidden,
        queries,
        cotangent,
        segment,
        clip_mask.reshape(1, block_rows),
        rewards.reshape(1, -1),
        seq_order.reshape(1, -1),
        fold(kv_weight),
        fold(moment_one),
        fold(moment_two),
        dec_hidden,
        dec_queries,
        kv_cache.reshape(requests, 2 * capacity, HD),
        cache_len,
    )
    *updated, dec_out = put(*results)
    return (*(value.reshape(kv_weight.shape) for value in updated), dec_out)


def solution(mesh):
    finer = Mesh(mesh.devices.reshape(4, 4, 4, 2, 4), AXES)
    in_specs = (
        P(FSDP_POOL, TENSOR),
        P(FSDP_POOL, TENSOR),
        P(FSDP_POOL, TENSOR),
        P(FSDP_POOL, None),
        P(FSDP_POOL),
        P(FSDP_POOL),
        P(FSDP_POOL),
        P(FSDP, None, TENSOR),
        P(FSDP, None, TENSOR),
        P(FSDP, None, TENSOR),
        P(FSDP_POOL, None, None),
        P(FSDP_POOL, None, TENSOR),
        P(FSDP_POOL, None, None, TENSOR),
        P(FSDP_POOL),
    )
    out_specs = (
        P(FSDP, None, TENSOR),
        P(FSDP, None, TENSOR),
        P(FSDP, None, TENSOR),
        P(FSDP_POOL, None, TENSOR),
    )
    return jax.shard_map(body, mesh=finer, in_specs=in_specs, out_specs=out_specs, check_vma=False)
```

time: 159 us -> 138 us (0.87)
  the two profiles are of different devices: /device:TPU:16 before, /device:TPU:2 now
where the time goes in v2:
time: 138 us
  Pallas kernels  137 us (99%)
    pallas_call x1, Pallas kernels, learner(): pl.pallas_call(learner_kernel, out_shape=(jax.ShapeDtypeStruct((640, HD),...  135 us

profile of v2, /device:TPU:2, one launch (start us, length us, event | category | flops | bytes accessed | tf_op | source)
XLA Modules:
  0.0 137.8 jit_solution(882595775529480173)
XLA Ops:
  0.6 134.9 %learner.1 = (f32[640,128]{1,0:T(8,128)}, f32[640,128]{1,0:T(8,128)}, f32[640,128]{1,0:T(8,128)}, bf16[8,4,640]{2,1,0:T(4,128)(2,1)}) custom-call(bf16[512,640]{1,0:T(8,128)(2,1)} %hidden.1, bf16[512,640]{1,0:T(8,128)(2,1)} %queries.1, bf16[512,640]{1,0:T(8,128)(2,1)} %cotangent.1, s32[1,512]{1,0:T(1,128)} %segment.1, s32[1,512]{1,0:T(1,128)} %bitcast.14, ...), custom_call_target="tpu_custom_call" | custom-call | tf_op jit(solution)/shard_map/learner/pallas_call | solution.py:725
  135.5 2.2 %put.1 = (f32[640,128]{1,0:T(8,128)}, f32[640,128]{1,0:T(8,128)}, f32[640,128]{1,0:T(8,128)}, bf16[8,4,640]{2,1,0:T(4,128)(2,1)}) custom-call(f32[640,128]{1,0:T(8,128)} %get-tuple-element.12.refs_0_, f32[640,128]{1,0:T(8,128)} %get-tuple-element.13.refs_1_, f32[640,128]{1,0:T(8,128)} %get-tuple-element.14.refs_2_, bf16[8,4,640]{2,1,0:T(4,128)(2,1)} %get-tuple-element.15.refs_3_), custom_call_target="tpu_custom_call" | custom-call | tf_op jit(solution)/shard_map/put/pallas_call | solution.py:783

commit v3 on v2

--- a/solution.py
+++ b/solution.py
@@ -294,6 +294,7 @@
     sum_two,
     land_z,
     grads,
+    results,
     local,
     sends,
     recvs,
@@ -336,7 +337,7 @@
     pl.semaphore_wait(barrier, len(peers))
 
     spot = Spots()
-    first_stat, first_line = spot.take(9), spot.take(13)
+    first_stat, first_line = spot.take(9), spot.take(26)
     stat_copies = []
     for k, (axis, index) in enumerate((("zh", zh), ("x", x), ("y", y))):
         stat_copies.append(
@@ -359,66 +360,74 @@
             copy.wait_recv()
         stat[k + 1] = (stat[k] + stat_land[k, 0]) + (stat_land[k, 1] + stat_land[k, 2])
 
-    def shard_right(d):
-        ref = tokens.at[zl - d, c]
-        return remote(ref, ref, sends, recvs, first_line + d, "zl", zl + 1)
-
-    def shard_left(d):
-        ref = tokens.at[zl + d, c]
-        return remote(ref, ref, sends, recvs, first_line + 3 + d, "zl", zl - 1)
-
-    def shard_across(j, k):
-        ref = tokens.at[j, c]
-        return remote(ref, ref, sends, recvs, first_line + 6 + k, "c", 1 - c)
-
-    def arrived(j, k):
-        ref = tokens.at[j, c]
-        remote(ref, ref, sends, recvs, first_line + k, "c", 1 - c).wait_recv()
-
-    def crossed(j, k):
-        ref = tokens.at[j, 1 - c]
-        remote(ref, ref, sends, recvs, first_line + 6 + k, "c", 1 - c).wait_recv()
+    span = hidden.shape[0] // 2
+
+    def half_of(j, core, q):
+        return tokens.at[j, core, pl.ds(span * q, span)]
+
+    def shard_right(d, q):
+        ref = half_of(zl - d, c, q)
+        return remote(ref, ref, sends, recvs, first_line + 2 * d + q, "zl", zl + 1)
+
+    def shard_left(d, q):
+        ref = half_of(zl + d, c, q)
+        return remote(ref, ref, sends, recvs, first_line + 6 + 2 * d + q, "zl", zl - 1)
+
+    def shard_across(j, k, q):
+        ref = half_of(j, c, q)
+        return remote(ref, ref, sends, recvs, first_line + 12 + 2 * k + q, "c", 1 - c)
+
+    def arrived(j, k, q):
+        ref = half_of(j, c, q)
+        remote(ref, ref, sends, recvs, first_line + 2 * k + q, "c", 1 - c).wait_recv()
+
+    def crossed(j, k, q):
+        ref = half_of(j, 1 - c, q)
+        remote(ref, ref, sends, recvs, first_line + 12 + 2 * k + q, "c", 1 - c).wait_recv()
 
     whole = pl.ds(0, 4)
     rows = GatherRows(w, (whole,), sends, recvs, spot)
     rows.deep.start()
     stat_start(0)
 
-    @pl.when(zl < 3)
-    def _():
-        shard_right(0).start()
-
-    @pl.when(zl > 0)
-    def _():
-        shard_left(0).start()
-
-    shard_across(zl, 0).start()
-
-    def pass_on(d):
+    for q in range(2):
+
+        @pl.when(zl < 3)
+        def _():
+            shard_right(0, q).start()
+
+        @pl.when(zl > 0)
+        def _():
+            shard_left(0, q).start()
+
+        shard_across(zl, 0, q).start()
+
+    def pass_on(d, q):
         @pl.when(zl >= d)
         def _():
-            arrived(zl - d, d - 1)
+            arrived(zl - d, d - 1, q)
             if d < 3:
 
                 @pl.when(zl < 3)
                 def _():
-                    shard_right(d).start()
-
-            shard_across(zl - d, d).start()
+                    shard_right(d, q).start()
+
+            shard_across(zl - d, d, q).start()
 
         @pl.when(zl + d <= 3)
         def _():
-            arrived(zl + d, 3 + d - 1)
+            arrived(zl + d, 3 + d - 1, q)
             if d < 3:
 
                 @pl.when(zl > 0)
                 def _():
-                    shard_left(d).start()
-
-            shard_across(zl + d, 3 + d).start()
+                    shard_left(d, q).start()
+
+            shard_across(zl + d, 3 + d, q).start()
 
     rows.deep.forward()
     stat_forward(0)
+    pass_on(1, 0)
     rows.deep.finish()
     rows.small[0].start()
     stat_finish(0)
@@ -428,7 +437,7 @@
     rows.large[0].start()
     stat_finish(1)
     stat_start(2)
-    pass_on(1)
+    pass_on(1, 1)
     rows.large[0].forward()
     stat_forward(2)
     rows.large[0].finish()
@@ -440,26 +449,28 @@
 
     acc[...] = jnp.zeros_like(acc)
 
-    def project(j):
+    def project(j, q):
+        here = pl.ds(span * q, span)
         for half in range(2):
-            acc[...] += jnp.dot(tokens[j, half], rows_of(w, j, half), preferred_element_type=f32)
-
-    crossed(zl, 0)
-    project(zl)
-
-    def take(d):
+            acc[here, :] += jnp.dot(tokens[j, half, here], rows_of(w, j, half), preferred_element_type=f32)
+
+    def take(d, q):
         @pl.when(zl >= d)
         def _():
-            crossed(zl - d, d)
-            project(zl - d)
+            crossed(zl - d, d, q)
+            project(zl - d, q)
 
         @pl.when(zl + d <= 3)
         def _():
-            crossed(zl + d, 3 + d)
-            project(zl + d)
-
-    pass_on(2)
-    take(1)
+            crossed(zl + d, 3 + d, q)
+            project(zl + d, q)
+
+    pass_on(2, 0)
+    for q in range(2):
+        crossed(zl, 0, q)
+        project(zl, q)
+    take(1, 0)
+    take(1, 1)
 
     for copy in late:
         copy.wait()
@@ -487,10 +498,9 @@
         top_sum[1, mine, :] = jnp.broadcast_to(jnp.sum(powers, axis=1, keepdims=True), (wide_rows, HD))
         cached[r] = pltpu.roll(powers, 1, 1)
 
-    pass_on(3)
-    take(2)
-    take(3)
-
+    pass_on(2, 1)
+    take(2, 0)
+    take(2, 1)
     sums = stat[3]
     means = sums[:, :64] / GROUP
     spreads = sums[:, 64:] / GROUP - means * means
@@ -509,12 +519,12 @@
 
     q_copy.wait()
     cot_copy.wait()
-    keys = acc[:, :HD].astype(bf16)
-    values = acc[:, HD:].astype(bf16)
     gacc[...] = jnp.zeros_like(gacc)
-    for i in range(block // HD):
+
+    def attend(i):
         here = slice(HD * i, HD * (i + 1))
         upto = HD * (i + 1)
+        keys, values = acc[:upto, :HD].astype(bf16), acc[:upto, HD:].astype(bf16)
         heads = [slice(HD * h, HD * (h + 1)) for h in range(RATIO)]
         q_rows = jnp.concatenate([q_in[here, h] for h in heads], axis=0)
         coef_here = coef_col[here]
@@ -525,16 +535,22 @@
         t_place = lax.broadcasted_iota(jnp.int32, (upto, HD), 1) + HD * i
         allowed = (seg_col[:upto] == seg_float[:, here]) & (u_place <= t_place)
         bias = jnp.where(allowed, 0.0, masked_score)
-        scores = lax.dot_general(keys[:upto], q_rows, contract_last, preferred_element_type=f32)
+        scores = lax.dot_general(keys, q_rows, contract_last, preferred_element_type=f32)
         scores = scores * scale + jnp.concatenate([bias] * RATIO, axis=1)
         top = jnp.max(scores, axis=0, keepdims=True)
         weights = jnp.exp(scores - top)
         attention = weights * (1.0 / jnp.sum(weights, axis=0, keepdims=True))
-        grad_prob = lax.dot_general(values[:upto], up_rows, contract_last, preferred_element_type=f32)
+        grad_prob = lax.dot_general(values, up_rows, contract_last, preferred_element_type=f32)
         inner = jnp.sum(attention * grad_prob, axis=0, keepdims=True)
         grad_score = (attention * (grad_prob - inner) * scale).astype(bf16)
         gacc[:upto, :HD] += jnp.dot(grad_score, q_rows, preferred_element_type=f32)
         gacc[:upto, HD:] += jnp.dot(attention.astype(bf16), up_rows, preferred_element_type=f32)
+
+    for q in range(2):
+        pass_on(3, q)
+        take(3, q)
+        attend(2 * q)
+        attend(2 * q + 1)
 
     grad_kv = gacc[...].astype(bf16)
 
@@ -639,6 +655,19 @@
     large[1].start()
     small[2].finish()
     large[2].start()
+    all_grads.finish()
+    for quarter in range(4):
+        for h in range(2):
+            rows_here, new, first, second = update(160 * quarter, h, grads[quarter, h])
+            results[0, rows_here, :] = new
+            results[1, rows_here, :] = first
+            results[2, rows_here, :] = second
+    outs = [
+        pltpu.make_async_copy(results.at[k], ref, local.at[7 + k])
+        for k, ref in enumerate((weight_out, one_out, two_out))
+    ]
+    for copy in outs:
+        copy.start()
     new_rows.deep.last()
     small[3].start()
     large[0].finish()
@@ -677,37 +706,32 @@
         for h in range(RATIO):
             dec_out[r, :, HD * h : HD * (h + 1)] = result[8 * h : 8 * h + steps].astype(bf16)
 
-    all_grads.finish()
-    for quarter in range(4):
-        for h in range(2):
-            rows_here, new, first, second = update(160 * quarter, h, grads[quarter, h])
-            weight_out[rows_here, :] = new
-            one_out[rows_here, :] = first
-            two_out[rows_here, :] = second
-
+    for copy in outs:
+        copy.wait()
     for group in stat_copies:
         for copy in group:
             copy.wait_send()
-    shard_across(zl, 0).wait_send()
-    for d in range(3):
-
-        @pl.when((zl >= d) & (zl < 3))
-        def _():
-            shard_right(d).wait_send()
-
-        @pl.when((zl + d <= 3) & (zl > 0))
-        def _():
-            shard_left(d).wait_send()
-
-    for d in (1, 2, 3):
-
-        @pl.when(zl >= d)
-        def _():
-            shard_across(zl - d, d).wait_send()
-
-        @pl.when(zl + d <= 3)
-        def _():
-            shard_across(zl + d, 3 + d).wait_send()
+    for q in range(2):
+        shard_across(zl, 0, q).wait_send()
+        for d in range(3):
+
+            @pl.when((zl >= d) & (zl < 3))
+            def _():
+                shard_right(d, q).wait_send()
+
+            @pl.when((zl + d <= 3) & (zl > 0))
+            def _():
+                shard_left(d, q).wait_send()
+
+        for d in (1, 2, 3):
+
+            @pl.when(zl >= d)
+            def _():
+                shard_across(zl - d, d, q).wait_send()
+
+            @pl.when(zl + d <= 3)
+            def _():
+                shard_across(zl + d, 3 + d, q).wait_send()
 
     for group in [rows, new_rows, all_grads, reduce_z] + one + two:
         group.drain()
@@ -731,7 +755,7 @@
             jax.ShapeDtypeStruct(dec_queries.shape, bf16),
         ),
         in_specs=[anywhere] * 3 + [vmem] * 5 + [anywhere] * 3 + [vmem, anywhere, pl.BlockSpec(memory_space=pltpu.SMEM)],
-        out_specs=(vmem,) * 4,
+        out_specs=(anywhere,) * 3 + (vmem,),
         scratch_shapes=[
             low(4, 2, block, features),
             low(*full),
@@ -761,7 +785,8 @@
             low(2, 4, 80, HD),
             low(6, 80, HD),
             wide(4, 2, 80, HD),
-            pltpu.SemaphoreType.DMA((7,)),
+            wide(3, 640, HD),
+            pltpu.SemaphoreType.DMA((10,)),
             pltpu.SemaphoreType.DMA((SEMS,)),
             pltpu.SemaphoreType.DMA((SEMS,)),
         ],

time: 138 us -> 132 us (0.957)
  Pallas kernels: 137 us -> 131 us
    pallas_call x1, Pallas kernels: 135 us -> 129 us  [learner(): pl.pallas_call(learner_kernel, out_shape=(jax.ShapeDtypeStruct((640, HD),...]
where the time goes in v3:
time: 132 us
  Pallas kernels  131 us (99%)
    pallas_call x1, Pallas kernels, learner(): pl.pallas_call(learner_kernel, out_shape=(jax.ShapeDtypeStruct((640, HD),...  129 us

profile of v3, /device:TPU:2, one launch (start us, length us, event | category | flops | bytes accessed | tf_op | source)
XLA Modules:
  0.0 132.0 jit_solution(6908273746015425717)
XLA Ops:
  0.6 129.1 %learner.1 = (f32[640,128]{1,0:T(8,128)}, f32[640,128]{1,0:T(8,128)}, f32[640,128]{1,0:T(8,128)}, bf16[8,4,640]{2,1,0:T(4,128)(2,1)}) custom-call(bf16[512,640]{1,0:T(8,128)(2,1)} %hidden.1, bf16[512,640]{1,0:T(8,128)(2,1)} %queries.1, bf16[512,640]{1,0:T(8,128)(2,1)} %cotangent.1, s32[1,512]{1,0:T(1,128)} %segment.1, s32[1,512]{1,0:T(1,128)} %bitcast.14, ...), custom_call_target="tpu_custom_call" | custom-call | tf_op jit(solution)/shard_map/learner/pallas_call | solution.py:749
  129.7 2.2 %put.1 = (f32[640,128]{1,0:T(8,128)}, f32[640,128]{1,0:T(8,128)}, f32[640,128]{1,0:T(8,128)}, bf16[8,4,640]{2,1,0:T(4,128)(2,1)}) custom-call(f32[640,128]{1,0:T(8,128)} %get-tuple-element.12.refs_0_, f32[640,128]{1,0:T(8,128)} %get-tuple-element.13.refs_1_, f32[640,128]{1,0:T(8,128)} %get-tuple-element.14.refs_2_, bf16[8,4,640]{2,1,0:T(4,128)(2,1)} %get-tuple-element.15.refs_3_), custom_call_target="tpu_custom_call" | custom-call | tf_op jit(solution)/shard_map/put/pallas_call | solution.py:808

commit v4 on v3

--- a/solution.py
+++ b/solution.py
@@ -20,7 +20,8 @@
 TENSOR = ("zl", "c")
 FSDP_POOL = ("x", "zh", "y")
 MESH = pl.DeviceIdType.MESH
-SEMS = 232
+SEMS = 256
+CUTS = 4
 
 beta_one = 0.9
 beta_two = 0.999
@@ -337,7 +338,7 @@
     pl.semaphore_wait(barrier, len(peers))
 
     spot = Spots()
-    first_stat, first_line = spot.take(9), spot.take(26)
+    first_stat, first_line = spot.take(9), spot.take(13 * CUTS)
     stat_copies = []
     for k, (axis, index) in enumerate((("zh", zh), ("x", x), ("y", y))):
         stat_copies.append(
@@ -360,37 +361,37 @@
             copy.wait_recv()
         stat[k + 1] = (stat[k] + stat_land[k, 0]) + (stat_land[k, 1] + stat_land[k, 2])
 
-    span = hidden.shape[0] // 2
-
-    def half_of(j, core, q):
+    span = hidden.shape[0] // CUTS
+
+    def cut_of(j, core, q):
         return tokens.at[j, core, pl.ds(span * q, span)]
 
     def shard_right(d, q):
-        ref = half_of(zl - d, c, q)
-        return remote(ref, ref, sends, recvs, first_line + 2 * d + q, "zl", zl + 1)
+        ref = cut_of(zl - d, c, q)
+        return remote(ref, ref, sends, recvs, first_line + CUTS * d + q, "zl", zl + 1)
 
     def shard_left(d, q):
-        ref = half_of(zl + d, c, q)
-        return remote(ref, ref, sends, recvs, first_line + 6 + 2 * d + q, "zl", zl - 1)
+        ref = cut_of(zl + d, c, q)
+        return remote(ref, ref, sends, recvs, first_line + CUTS * (3 + d) + q, "zl", zl - 1)
 
     def shard_across(j, k, q):
-        ref = half_of(j, c, q)
-        return remote(ref, ref, sends, recvs, first_line + 12 + 2 * k + q, "c", 1 - c)
+        ref = cut_of(j, c, q)
+        return remote(ref, ref, sends, recvs, first_line + CUTS * (6 + k) + q, "c", 1 - c)
 
     def arrived(j, k, q):
-        ref = half_of(j, c, q)
-        remote(ref, ref, sends, recvs, first_line + 2 * k + q, "c", 1 - c).wait_recv()
+        ref = cut_of(j, c, q)
+        remote(ref, ref, sends, recvs, first_line + CUTS * k + q, "c", 1 - c).wait_recv()
 
     def crossed(j, k, q):
-        ref = half_of(j, 1 - c, q)
-        remote(ref, ref, sends, recvs, first_line + 12 + 2 * k + q, "c", 1 - c).wait_recv()
+        ref = cut_of(j, 1 - c, q)
+        remote(ref, ref, sends, recvs, first_line + CUTS * (6 + k) + q, "c", 1 - c).wait_recv()
 
     whole = pl.ds(0, 4)
     rows = GatherRows(w, (whole,), sends, recvs, spot)
     rows.deep.start()
     stat_start(0)
 
-    for q in range(2):
+    for q in range(CUTS):
 
         @pl.when(zl < 3)
         def _():
@@ -399,8 +400,6 @@
         @pl.when(zl > 0)
         def _():
             shard_left(0, q).start()
-
-        shard_across(zl, 0, q).start()
 
     def pass_on(d, q):
         @pl.when(zl >= d)
@@ -412,8 +411,6 @@
                 def _():
                     shard_right(d, q).start()
 
-            shard_across(zl - d, d, q).start()
-
         @pl.when(zl + d <= 3)
         def _():
             arrived(zl + d, 3 + d - 1, q)
@@ -423,25 +420,41 @@
                 def _():
                     shard_left(d, q).start()
 
+    def hand_over(d, q):
+        @pl.when(zl >= d)
+        def _():
+            shard_across(zl - d, d, q).start()
+
+        @pl.when(zl + d <= 3)
+        def _():
             shard_across(zl + d, 3 + d, q).start()
 
     rows.deep.forward()
     stat_forward(0)
     pass_on(1, 0)
+    pass_on(1, 1)
     rows.deep.finish()
     rows.small[0].start()
     stat_finish(0)
     stat_start(1)
     stat_forward(1)
+    pass_on(1, 2)
     rows.small[0].finish()
     rows.large[0].start()
     stat_finish(1)
     stat_start(2)
-    pass_on(1, 1)
+    pass_on(1, 3)
+
+    for q in range(CUTS):
+        shard_across(zl, 0, q).start()
+        hand_over(1, q)
     rows.large[0].forward()
     stat_forward(2)
     rows.large[0].finish()
     stat_finish(2)
+    for q in range(CUTS):
+        pass_on(2, q)
+        hand_over(2, q)
 
     def rows_of(source, j, half):
         pieces = [source[h, j, pl.ds(2 * half, 2)].reshape(640, HD) for h in range(2)]
@@ -449,28 +462,24 @@
 
     acc[...] = jnp.zeros_like(acc)
 
-    def project(j, q):
-        here = pl.ds(span * q, span)
+    def project(j, here):
         for half in range(2):
             acc[here, :] += jnp.dot(tokens[j, half, here], rows_of(w, j, half), preferred_element_type=f32)
 
-    def take(d, q):
+    everything = pl.ds(0, hidden.shape[0])
+
+    def take(d):
         @pl.when(zl >= d)
         def _():
-            crossed(zl - d, d, q)
-            project(zl - d, q)
+            for q in range(CUTS):
+                crossed(zl - d, d, q)
+            project(zl - d, everything)
 
         @pl.when(zl + d <= 3)
         def _():
-            crossed(zl + d, 3 + d, q)
-            project(zl + d, q)
-
-    pass_on(2, 0)
-    for q in range(2):
-        crossed(zl, 0, q)
-        project(zl, q)
-    take(1, 0)
-    take(1, 1)
+            for q in range(CUTS):
+                crossed(zl + d, 3 + d, q)
+            project(zl + d, everything)
 
     for copy in late:
         copy.wait()
@@ -498,9 +507,11 @@
         top_sum[1, mine, :] = jnp.broadcast_to(jnp.sum(powers, axis=1, keepdims=True), (wide_rows, HD))
         cached[r] = pltpu.roll(powers, 1, 1)
 
-    pass_on(2, 1)
-    take(2, 0)
-    take(2, 1)
+    for q in range(CUTS):
+        crossed(zl, 0, q)
+    project(zl, everything)
+    take(1)
+    take(2)
     sums = stat[3]
     means = sums[:, :64] / GROUP
     spreads = sums[:, 64:] / GROUP - means * means
@@ -546,11 +557,22 @@
         gacc[:upto, :HD] += jnp.dot(grad_score, q_rows, preferred_element_type=f32)
         gacc[:upto, HD:] += jnp.dot(attention.astype(bf16), up_rows, preferred_element_type=f32)
 
-    for q in range(2):
+    for q in range(CUTS):
+        here = pl.ds(span * q, span)
         pass_on(3, q)
-        take(3, q)
-        attend(2 * q)
-        attend(2 * q + 1)
+        hand_over(3, q)
+
+        @pl.when(zl == 3)
+        def _():
+            crossed(0, 3, q)
+            project(0, here)
+
+        @pl.when(zl == 0)
+        def _():
+            crossed(3, 6, q)
+            project(3, here)
+
+        attend(q)
 
     grad_kv = gacc[...].astype(bf16)
 
@@ -586,7 +608,10 @@
             )
         )
         two_to.append((sum_two.at[0, p], sum_two.at[1, p]))
-    reduce_z = ring("zh", lambda j, h: sum_two.at[h, j], lambda k, h: land_z.at[k])
+    first_z = spot.take(3)
+    to_zh = [
+        remote(sum_two.at[:, p], land_z.at[n], sends, recvs, first_z + n, "zh", p) for n, p in enumerate(order_of[:3])
+    ]
 
     outer(lax.div(far, 2))
     one[0].start()
@@ -601,19 +626,25 @@
     one[1].finish(one_to[1])
     two[1].start()
     two[0].finish(two_to[0])
-    reduce_z.start_far()
+    to_zh[0].start()
     one[2].forward()
     one[2].finish(one_to[2])
     two[2].start()
     one[3].forward()
     two[1].finish(two_to[1])
+    to_zh[1].start()
     two[2].finish(two_to[2])
-    reduce_z.start_near()
+    to_zh[2].start()
     one[3].finish(one_to[3])
     two[3].start()
-    reduce_z.forward()
     two[3].finish(two_to[3])
-    reduce_z.finish(lambda h: grads.at[y, h])
+    for copy in to_zh:
+        copy.wait_recv()
+    for h in range(2):
+        total = sum_two[h, zh].astype(f32)
+        for n in range(3):
+            total = total + land_z[n, h].astype(f32)
+        grads[y, h] = total
 
     def update(start, h, grad):
         rows_here = pl.ds(start + h, 80, stride=2)
@@ -711,7 +742,7 @@
     for group in stat_copies:
         for copy in group:
             copy.wait_send()
-    for q in range(2):
+    for q in range(CUTS):
         shard_across(zl, 0, q).wait_send()
         for d in range(3):
 
@@ -733,7 +764,9 @@
             def _():
                 shard_across(zl + d, 3 + d, q).wait_send()
 
-    for group in [rows, new_rows, all_grads, reduce_z] + one + two:
+    for copy in to_zh:
+        copy.wait_send()
+    for group in [rows, new_rows, all_grads] + one + two:
         group.drain()
 
 
@@ -783,7 +816,7 @@
             low(4, 3, 80, HD),
             low(4, 3, 80, HD),
             low(2, 4, 80, HD),
-            low(6, 80, HD),
+            low(3, 2, 80, HD),
             wide(4, 2, 80, HD),
             wide(3, 640, HD),
             pltpu.SemaphoreType.DMA((10,)),

time: 132 us -> 131 us (level)
  no operation moved by 1% of the time
where the time goes in v4:
time: 131 us
  Pallas kernels  130 us (99%)
    pallas_call x1, Pallas kernels, learner(): pl.pallas_call(learner_kernel, out_shape=(jax.ShapeDtypeStruct((640, HD),...  128 us

profile of v4, /device:TPU:2, one launch (start us, length us, event | category | flops | bytes accessed | tf_op | source)
XLA Modules:
  0.0 130.8 jit_solution(8575573940469931483)
XLA Ops:
  0.6 127.9 %learner.1 = (f32[640,128]{1,0:T(8,128)}, f32[640,128]{1,0:T(8,128)}, f32[640,128]{1,0:T(8,128)}, bf16[8,4,640]{2,1,0:T(4,128)(2,1)}) custom-call(bf16[512,640]{1,0:T(8,128)(2,1)} %hidden.1, bf16[512,640]{1,0:T(8,128)(2,1)} %queries.1, bf16[512,640]{1,0:T(8,128)(2,1)} %cotangent.1, s32[1,512]{1,0:T(1,128)} %segment.1, s32[1,512]{1,0:T(1,128)} %bitcast.14, ...), custom_call_target="tpu_custom_call" | custom-call | tf_op jit(solution)/shard_map/learner/pallas_call | solution.py:782
  128.5 2.2 %put.1 = (f32[640,128]{1,0:T(8,128)}, f32[640,128]{1,0:T(8,128)}, f32[640,128]{1,0:T(8,128)}, bf16[8,4,640]{2,1,0:T(4,128)(2,1)}) custom-call(f32[640,128]{1,0:T(8,128)} %get-tuple-element.12.refs_0_, f32[640,128]{1,0:T(8,128)} %get-tuple-element.13.refs_1_, f32[640,128]{1,0:T(8,128)} %get-tuple-element.14.refs_2_, bf16[8,4,640]{2,1,0:T(4,128)(2,1)} %get-tuple-element.15.refs_3_), custom_call_target="tpu_custom_call" | custom-call | tf_op jit(solution)/shard_map/put/pallas_call | solution.py:841
